TPU v7x, 32 devices: a whole 2x2x4 slice. The times are simulated.
32 devices in a mesh: row: 8 (over y, x, core), col: 4 (over z).
Axes of the slice: x: 2, y: 2, z: 4, core: 2. Of those that a mesh axis runs over, the one named last changes fastest.
Arguments:
- expression: bfloat16 [4096, 1024], P(('row', 'col')), may hold values from -200 to 200, as said below
- powers: int32 [10], replicated, may hold values from 1 to 20
Outputs:
- log_degree: float32 [10, 4096], P(None, ('row', 'col'))
- degree_freq: float32 [10, 10], replicated
- fit_slope: float32 [10], replicated
- mean_log: float32 [10], replicated
Inputs may be any that keep to these rules, and one draw needn't show every extreme that they name: Finite expression values.
All inputs are finite; a program needn't handle non-finite values.
Results may differ from a plain program's by a relative error of at most 0.0003.
Values may be sent and summed in bfloat16 or wider, within the bound.
No kernel may reach another device: no remote copies, remote signals or barrier semaphores. Data moves between devices by JAX's collectives and lax.ppermute only.
A program may use at most 64 MiB of HBM per device.

v0:
```python
import jax
import jax.numpy as jnp
from jax import lax
from jax.sharding import PartitionSpec as P

BINS = 10


def gene_stats(genes):
    values = genes.astype(jnp.float32)
    gene_mean = jnp.mean(values, axis=1)
    centred = values - gene_mean[:, None]
    gene_inv = lax.rsqrt(jnp.mean(centred * centred, axis=1) + 1e-06)
    return (gene_mean, gene_inv)


def add_slice(totals, addend, start):
    current = lax.dynamic_slice_in_dim(totals, start, addend.shape[1], 1)
    return lax.dynamic_update_slice_in_dim(totals, current + addend, start, 1)


def block_sums(left_genes, right_genes, exponents, row_list, carry, left_start):
    row_count = left_genes.shape[0]
    block_rows = 256
    samples = left_genes.shape[1]
    left_mean, left_inv = gene_stats(left_genes)
    right_mean, right_inv = gene_stats(right_genes)

    def one_block(block_index, totals):
        row_totals, column_totals = totals
        offset = block_index * block_rows
        row_block = lax.dynamic_slice_in_dim(left_genes, offset, block_rows, 0)
        block_mean = lax.dynamic_slice_in_dim(left_mean, offset, block_rows, 0)
        block_inv = lax.dynamic_slice_in_dim(left_inv, offset, block_rows, 0)
        raw = lax.dot_general(
            row_block, right_genes, (((1,), (1,)), ((), ())), preferred_element_type=jnp.float32
        )
        pearson = (
            (raw / samples - block_mean[:, None] * right_mean[None, :])
            * block_inv[:, None]
            * right_inv[None, :]
        )
        log_abs = jnp.log(jnp.abs(pearson))
        row_parts = []
        for power_index in row_list:
            row_parts.append(jnp.sum(jnp.exp(exponents[power_index] * log_abs), axis=1))
        if row_parts:
            row_totals = add_slice(row_totals, jnp.stack(row_parts), left_start + offset)
        return (row_totals, column_totals)

    return lax.fori_loop(0, row_count // block_rows, one_block, carry)


def on_device(expression, powers):
    exponents = powers.astype(jnp.float32)
    npower = powers.shape[0]
    local_genes = expression.shape[0]
    row_width = local_genes * lax.axis_size("col")
    column_width = local_genes * lax.axis_size("row")
    row_list = list(range(npower))
    col_list = []
    initial = (
        jnp.zeros((len(row_list), row_width), jnp.float32),
        jnp.zeros((max(len(col_list), 1), column_width), jnp.float32),
    )
    left_genes = lax.all_gather(expression, "col", axis=0, tiled=True)
    row_totals, column_totals = block_sums(
        left_genes,
        lax.all_gather(expression, "row", axis=0, tiled=True),
        exponents,
        row_list,
        initial,
        0,
    )
    degree = lax.psum_scatter(row_totals, "col", scatter_dimension=1, tiled=True)
    peak = lax.pmax(jnp.max(degree, axis=1), ("row", "col"))
    position = jnp.clip(BINS * degree / peak[:, None] - 0.5, 0.0, BINS - 1.0)
    centres = jnp.arange(BINS, dtype=jnp.float32)
    weights = jnp.maximum(0.0, 1.0 - jnp.abs(position[:, :, None] - centres[None, None, :]))
    freq_total, degree_total = lax.psum(
        (jnp.sum(weights, axis=1), jnp.sum(degree, axis=1)), ("row", "col")
    )
    genes_all = local_genes * lax.axis_size("row") * lax.axis_size("col")
    degree_freq = freq_total / genes_all
    mean_log = jnp.log10(degree_total / genes_all)
    xfit = jnp.log10((centres[None, :] + 0.5) * peak[:, None] / BINS)
    yfit = jnp.log10(degree_freq + 1.0 / genes_all)
    xdev = xfit - jnp.mean(xfit, axis=1, keepdims=True)
    ydev = yfit - jnp.mean(yfit, axis=1, keepdims=True)
    fit_slope = jnp.sum(xdev * ydev, axis=1) / jnp.sum(xdev * xdev, axis=1)
    return (jnp.log10(degree), degree_freq, fit_slope, mean_log)


def solution(mesh):
    return jax.shard_map(
        on_device,
        mesh=mesh,
        in_specs=(P(("row", "col"), None), P()),
        out_specs=(P(None, ("row", "col")), P(), P(), P()),
        check_vma=False,
    )
```

profile of v0, /device:TPU:0, one launch (start us, length us, event | category | flops | bytes accessed | tf_op | source)
XLA Modules:
  0.0 201.4 jit_solution(1471055572352535315)
XLA Ops:
  7.2 0.0 all-gather.3.cloned.1.call-start
  7.2 0.7 all-gather.3.cloned.1.call-update
  7.9 0.0 all-gather.5.cloned.1.call-start
  7.9 0.7 all-gather.5.cloned.1.call-update
  8.6 0.0 reduce-scatter.2.cloned.1.call-start
  8.7 0.7 convert_element_type.9
  9.4 30.9 %all-gather.3.cloned.1.call-done = bf16[512,1024]{1,0:T(8,128)(2,1)} async-done(((bf16[128,1024]{1,0:T(8,128)(2,1)}), bf16[512,1024]{1,0:T(8,128)(2,1)}) %all-gather.3.cloned.1.call-update) | async-done | bytes 1048592 | tf_op jit(solution)/shard_map/all_gather | solution.py:66
  40.3 1.4 convert_reduce_fusion.1
  41.7 1.6 fusion.10
  43.4 26.0 %all-gather.5.cloned.1.call-done = bf16[1024,1024]{1,0:T(8,128)(2,1)} async-done(((bf16[128,1024]{1,0:T(8,128)(2,1)}), bf16[1024,1024]{1,0:T(8,128)(2,1)}) %all-gather.5.cloned.1.call-update) | async-done | bytes 2097168 | tf_op jit(solution)/shard_map/all_gather | solution.py:69
  69.4 0.0 copy-start
  69.4 0.0 copy-start.1
  69.4 2.1 %convert_reduce_fusion = f32[1024]{0:T(1024)S(1)} fusion(bf16[1024,1024]{1,0:T(8,128)(2,1)} %all-gather.5.cloned.1.call-done), kind=kLoop, calls=%fused_computation.20 | loop fusion | flops 2096128 | bytes 2101248 | tf_op jit(solution)/shard_map/reduce_sum | solution.py:11
  71.5 0.1 copy-done
  71.6 0.7 fusion.8
  72.3 0.0 copy-done.1
  72.3 19.4 %while.13 = (s32[]{:T(128)}, f32[10,512]{1,0:T(8,128)S(1)}, f32[10]{0:T(128)S(1)}, bf16[512,1024]{1,0:T(8,128)(2,1)S(1)}, bf16[1024,1024]{1,0:T(8,128)(2,1)S(1)}...) while((s32[]{:T(128)}, f32[10,512]{1,0:T(8,128)S(1)}, ...), condition=%wide.region_15.0_spmd, body=%wide.region_4.0_spmd.sunk | while | flops 543686656 | bytes 2715955 | solution.py:51
  72.3 0.1 dynamic_slice.39
  72.4 0.1 dynamic_slice.40
  72.5 0.7 fusion.20
  73.2 8.8 %exponential_reduce_fusion.11 = (f32[256]{0:T(256)S(1)}, f32[256]{0:T(256)S(1)}, f32[256]{0:T(256)S(1)}, f32[256]{0:T(256)S(1)}, f32[256]{0:T(256)S(1)}, /*index...) fusion(f32[]{:T(128)} %bitcast.43, f32[]{:T(128)} %bitcast.44, ...), kind=kOutput, calls=%fused_computation.6.clone.1 | convolution fusion | flops 543684096 | bytes 2641964 | tf_op jit(solution)/shard_map/while/body/eval_jaxpr/dot_general | solution.py:35
  81.9 0.1 stack.78
  82.0 0.1 dynamic_slice.39
  82.1 0.1 dynamic_slice.40
  82.2 0.7 fusion.20
  82.9 8.8 %exponential_reduce_fusion.11 = (f32[256]{0:T(256)S(1)}, f32[256]{0:T(256)S(1)}, f32[256]{0:T(256)S(1)}, f32[256]{0:T(256)S(1)}, f32[256]{0:T(256)S(1)}, /*index...) fusion(f32[]{:T(128)} %bitcast.43, f32[]{:T(128)} %bitcast.44, ...), kind=kOutput, calls=%fused_computation.6.clone.1 | convolution fusion | flops 543684096 | bytes 2641964 | tf_op jit(solution)/shard_map/while/body/eval_jaxpr/dot_general | solution.py:35
  91.6 0.1 stack.78
  91.7 0.0 copy-start.2
  91.7 0.6 copy-done.2
  92.3 0.0 reduce-scatter.2.cloned.1.call-update
  92.4 19.3 %reduce-scatter.2.cloned.1.call-done = f32[10,128]{1,0:T(8,128)} async-done(((f32[10,512]{1,0:T(8,128)}), f32[10,128]{1,0:T(8,128)}) %reduce-scatter.2.cloned.1.call-update) | async-done | bytes 5136 | tf_op jit(solution)/shard_map/reduce_scatter | solution.py:75
  111.7 0.8 fusion.14
  112.5 38.4 %pmax.7 = f32[10]{0:T(128)S(1)} all-reduce(f32[10]{0:T(128)S(1)} %get-tuple-element.170), channel_id=1, replica_groups=mesh['row'=8,'col'=4] {'row','col'}, use_global_device_ids=true, to_apply=%region_18.0 | all-reduce | flops 10 | bytes 80 | tf_op jit(solution)/shard_map/pmax | solution.py:76
  150.9 1.3 add_clamp_fusion
  152.2 0.1 maximum_reduce_fusion
  152.3 40.9 %all-reduce = (f32[10,10]{1,0:T(8,128)S(1)}, f32[10]{0:T(128)S(1)}) all-reduce(f32[10,10]{1,0:T(8,128)S(1)} %maximum_reduce_fusion, f32[10]{0:T(128)S(1)} %get-tuple-element.169), channel_id=1, replica_groups=mesh['row'=8,'col'=4] {'row','col'}, use_global_device_ids=true, to_apply=%region_20.21 | all-reduce | flops 110 | bytes 880 | tf_op jit(solution)/shard_map/psum | solution.py:80
  193.3 0.1 fusion.13
  193.4 0.0 copy-start.3
  193.4 0.2 fusion.12
  193.6 0.5 log_multiply_fusion.3
  194.1 0.2 multiply_reduce_fusion
  194.3 0.5 div.61
  194.9 0.0 copy-done.3
  (10 shorter events, 0.1 us)
Async XLA Ops:
  7.2 33.1 %all-gather.3.cloned.1.call-start = ((), (), s32[]{:S(2)}) async-start(), calls=%async_computation.1 | async-start | bytes 1310720 | tf_op jit(solution)/shard_map/all_gather | solution.py:66
  7.9 61.5 %all-gather.5.cloned.1.call-start = ((), (), s32[]{:S(2)}) async-start(), calls=%async_computation.2 | async-start | bytes 2359296 | tf_op jit(solution)/shard_map/all_gather | solution.py:69
  8.6 103.0 %reduce-scatter.2.cloned.1.call-start = ((), (), s32[]{:S(2)}) async-start(), calls=%async_computation.3 | async-start | bytes 40960 | tf_op jit(solution)/shard_map/reduce_scatter | solution.py:75
  69.4 2.2 %copy-start = (bf16[1024,1024]{1,0:T(8,128)(2,1)S(1)}, bf16[1024,1024]{1,0:T(8,128)(2,1)}, u32[]{:S(2)}) copy-start(bf16[1024,1024]{1,0:T(8,128)(2,1)} %all-gather.5.cloned.1.call-done) | copy-start | bytes 6291460
  69.4 2.9 %copy-start.1 = (bf16[512,1024]{1,0:T(8,128)(2,1)S(1)}, bf16[512,1024]{1,0:T(8,128)(2,1)}, u32[]{:S(2)}) copy-start(bf16[512,1024]{1,0:T(8,128)(2,1)} %all-gather.3.cloned.1.call-done) | copy-start | bytes 3145732
  91.7 0.6 copy-start.2
  193.4 1.5 copy-start.3
Sparse Core Ops, SparseCore 0:
  9.5 30.6 all-gather.2
  42.2 27.1 all-gather.4
  92.5 19.1 reduce-scatter.1
where the time goes:
time: 202 us; the launch traced here: 201 us
  blocking collectives  79.4 us (39%)
  waiting for transfers between devices  77.6 us (38%)
  matrix products  17.6 us (9%)
  between operations  13.8 us (7%)
  other arithmetic  10.3 us (5%)
  local copies, waits for them, and re-layouts  2.49 us (1%)
    psum x1, blocking collectives, on_device(): lax.psum((jnp.sum(weights, axis=1), jnp.sum(degree, axis=1)), ('row', 'co...  40.9 us
    pmax x1, blocking collectives, on_device(): peak = lax.pmax(jnp.max(degree, axis=1), ('row', 'col'))  38.4 us
    all_gather x1, waiting for transfers between devices, on_device(): left_genes = lax.all_gather(expression, 'col', axis=0, tiled=True)  30.9 us
    all_gather x1, waiting for transfers between devices, on_device(): lax.all_gather(expression, 'row', axis=0, tiled=True)  26 us
    reduce_scatter x1, waiting for transfers between devices, on_device(): lax.psum_scatter(row_totals, 'col', scatter_dimension=1, tiled=True)  19.3 us
    dot_general x2, matrix products, one_block(): lax.dot_general(row_block, right_genes, (((1,), (1,)), ((), ())), preferr...  17.6 us
  transfers between devices with their start and end apart: 3, of which 3 were waited for; matrix products, arithmetic and copies ran while one was open for 2% of the time, Pallas kernels for 0%

commit v1 on v0

v1 whole, which is shorter than its diff:
```python
import functools

import jax
import jax.numpy as jnp
from jax import lax
from jax.experimental import pallas as pl
from jax.experimental.pallas import tpu as pltpu
from jax.sharding import PartitionSpec as P


BINS = 10
AXES = ("row", "col")
LOG2E = 1.4426950408889634
LOG10E = 0.4342944819032518
TILE = 8
VMEM_LIMIT = 20 * 2**20


def gene_stats(genes):
    values = genes.astype(jnp.float32)
    samples = values.shape[1]
    mean = jnp.sum(values, axis=1, keepdims=True) * (1.0 / samples)
    centred = values - mean
    var = jnp.sum(centred * centred, axis=1, keepdims=True) * (1.0 / samples)
    return mean, lax.rsqrt(var + 1e-06)


def as_row(column):
    genes = column.shape[0]
    return jnp.transpose(jnp.broadcast_to(column, (genes, genes)))[0:1, :]


def vmem_spec():
    return pl.BlockSpec(memory_space=pltpu.VMEM)


def smem_spec():
    return pl.BlockSpec(memory_space=pltpu.SMEM)


def stats_kernel(count, *refs):
    out = refs[-1]
    for b in range(count):
        genes, samples = refs[b].shape
        mean, inv = gene_stats(refs[b][...])
        out[b, 0] = jnp.broadcast_to(mean * samples, (genes, genes))
        out[b, 1] = jnp.broadcast_to(inv * (1.0 / samples), (genes, genes))


def stats(blocks):
    genes = blocks[0].shape[0]
    return pl.pallas_call(
        functools.partial(stats_kernel, len(blocks)),
        out_shape=jax.ShapeDtypeStruct((len(blocks), 2, genes, genes), jnp.float32),
        in_specs=[vmem_spec()] * len(blocks),
        out_specs=vmem_spec(),
        compiler_params=pltpu.CompilerParams(vmem_limit_bytes=VMEM_LIMIT),
        cost_estimate=pl.CostEstimate(
            flops=400000 * len(blocks), bytes_accessed=400000 * len(blocks), transcendentals=0
        ),
    )(*blocks)


def add_powers(powers, lane_refs, sub_refs, stat_refs, raw, emit):
    npower = powers.shape[0]
    genes, _ = lane_refs[0].shape
    chunk = 32
    scales = [powers[p].astype(jnp.float32) * LOG2E for p in range(npower)]

    def one_lane_block(a, lane_ref):
        mean, inv = gene_stats(lane_ref[...])
        lane_mean, lane_inv = as_row(mean), as_row(inv)
        for b, sub_ref in enumerate(sub_refs):
            raw[b] = lax.dot_general(
                sub_ref[...],
                lane_ref[...],
                (((1,), (1,)), ((), ())),
                preferred_element_type=jnp.float32,
            )
        sums = [jnp.zeros((TILE, genes), jnp.float32) for _ in range(npower)]
        for b in range(len(sub_refs)):
            for c in range(0, genes, chunk):
                part = slice(c, c + chunk)
                pearson = (
                    (raw[b, part, :] - stat_refs[b][0, part, :] * lane_mean)
                    * stat_refs[b][1, part, :]
                    * lane_inv
                )
                log_abs = jnp.log(jnp.abs(pearson))
                for p in range(npower):
                    term = jnp.exp2(log_abs * scales[p])
                    sums[p] = sums[p] + jnp.sum(
                        term.reshape(chunk // TILE, TILE, genes), axis=0
                    )
        emit(a, [jnp.sum(total, axis=0, keepdims=True) for total in sums])

    for a, lane_ref in enumerate(lane_refs):
        one_lane_block(a, lane_ref)


def early_kernel(lane_count, sub_count, stat_sizes, *refs):
    powers, refs = refs[0], refs[1:]
    lanes, refs = refs[:lane_count], refs[lane_count:]
    subs, refs = refs[:sub_count], refs[sub_count:]
    stat_refs = [refs[i].at[j] for i, size in enumerate(stat_sizes) for j in range(size)]
    out, raw = refs[-2:]

    def emit(a, rows):
        for p, row in enumerate(rows):
            out[a, p : p + 1, :] = row

    add_powers(powers, lanes, subs, stat_refs, raw, emit)


def late_kernel(lane_count, sub_count, stat_sizes, *refs):
    powers, place, refs = refs[0], refs[1], refs[2:]
    lanes, refs = refs[:lane_count], refs[lane_count:]
    subs, refs = refs[:sub_count], refs[sub_count:]
    stat_refs = [refs[i].at[j] for i, size in enumerate(stat_sizes) for j in range(size)]
    prior, out, raw = refs[-3:]
    npower = powers.shape[0]
    genes = lanes[0].shape[0]
    prior_count = prior.shape[0]
    slots = prior_count + lane_count
    full, rest = npower // TILE, npower % TILE
    mine = place[0]
    tail_tiles = out.shape[0] - slots * full
    sublane = lax.broadcasted_iota(jnp.int32, (TILE, genes), 0)
    tail = [jnp.zeros((TILE, genes), jnp.float32) for _ in range(tail_tiles)]

    def emit(slot, rows):
        where = slot ^ mine
        for f in range(full):
            for r in range(TILE):
                out[f * slots + where, r : r + 1, :] = rows[f * TILE + r]
        for q in range(rest):
            for t in range(tail_tiles):
                hit = sublane + t * TILE == q * slots + where
                tail[t] = jnp.where(hit, rows[full * TILE + q], tail[t])

    add_powers(powers, lanes, subs, stat_refs, raw, lambda a, rows: emit(prior_count + a, rows))
    for s in range(prior_count):
        emit(s, [prior[s, p : p + 1, :] for p in range(npower)])
    for t in range(tail_tiles):
        out[slots * full + t] = tail[t]


def tile_count(npower, slots):
    return slots * (npower // TILE) + -(-(npower % TILE) * slots // TILE)


def degrees(powers, lane_blocks, sub_blocks, sub_stats, place=None, prior=None):
    npower = powers.shape[0]
    genes, samples = lane_blocks[0].shape
    lane_count, sub_count = len(lane_blocks), len(sub_blocks)
    pairs = lane_count * sub_count * genes * genes
    operands = list(lane_blocks) + list(sub_blocks) + list(sub_stats)
    scalars = [powers]
    sizes = [array.shape[0] for array in sub_stats]
    if prior is None:
        kernel = early_kernel
        out_shape = (lane_count, npower, genes)
    else:
        kernel = late_kernel
        operands, scalars = operands + [prior], [powers, place]
        out_shape = (tile_count(npower, prior.shape[0] + lane_count), TILE, genes)
    return pl.pallas_call(
        functools.partial(kernel, lane_count, sub_count, sizes),
        out_shape=jax.ShapeDtypeStruct(out_shape, jnp.float32),
        in_specs=[smem_spec()] * len(scalars) + [vmem_spec()] * len(operands),
        out_specs=vmem_spec(),
        scratch_shapes=[pltpu.VMEM((sub_count, genes, genes), jnp.float32)],
        compiler_params=pltpu.CompilerParams(vmem_limit_bytes=VMEM_LIMIT),
        cost_estimate=pl.CostEstimate(
            flops=2 * pairs * samples,
            bytes_accessed=2 * genes * samples * (lane_count + sub_count),
            transcendentals=pairs * (npower + 1),
        ),
    )(*scalars, *operands)


def fit_kernel(npower, slots, place, deg, log_degree, degree_freq, fit_slope, mean_log):
    groups, tiles, _, genes = deg.shape
    full, rest = npower // TILE, npower % TILE
    total_genes = groups * slots * genes
    inv_genes = 1.0 / total_genes
    mine, start = place[0], place[1]
    tail = tiles - slots * full
    sublane = lax.broadcasted_iota(jnp.int32, (TILE, genes), 0)
    lane = lax.broadcasted_iota(jnp.int32, (TILE, genes), 1)
    slope_row, mean_row = 0.0, 0.0

    def hat(value, inverse, counts):
        position = jnp.clip(BINS * value * inverse - 0.5, 0.0, BINS - 1.0)
        return [
            count + jnp.maximum(0.0, 1.0 - jnp.abs(position - b)) for b, count in enumerate(counts)
        ]

    def line(peak, freq, total):
        used = lane < BINS
        centre = lane.astype(jnp.float32) + 0.5
        xfit = jnp.where(used, jnp.log(centre * peak * (1.0 / BINS)) * LOG10E, 0.0)
        yfit = jnp.where(used, jnp.log(freq + inv_genes) * LOG10E, 0.0)
        xdev = jnp.where(used, xfit - jnp.sum(xfit, axis=1, keepdims=True) * (1.0 / BINS), 0.0)
        ydev = jnp.where(used, yfit - jnp.sum(yfit, axis=1, keepdims=True) * (1.0 / BINS), 0.0)
        slope = jnp.sum(xdev * ydev, axis=1, keepdims=True) / jnp.sum(
            xdev * xdev, axis=1, keepdims=True
        )
        return slope, jnp.log(total * inv_genes) * LOG10E

    def on_lanes(counts):
        freq = jnp.zeros((TILE, genes), jnp.float32)
        for b in range(BINS):
            freq = jnp.where(lane == b, counts[b] * inv_genes, freq)
        return freq

    zero = jnp.zeros((TILE, genes), jnp.float32)
    for f in range(full):
        top = deg[0, f * slots]
        for g in range(groups):
            for s in range(slots):
                top = jnp.maximum(top, deg[g, f * slots + s])
        peak = jnp.max(top, axis=1, keepdims=True)
        inverse = 1.0 / peak
        total, counts = zero, [zero] * BINS
        for g in range(groups):
            for s in range(slots):
                value = deg[g ^ start, f * slots + s]
                total = total + value
                counts = hat(value, inverse, counts)
        freq = on_lanes([jnp.sum(count, axis=1, keepdims=True) for count in counts])
        slope, mean = line(peak, freq, jnp.sum(total, axis=1, keepdims=True))
        log_degree[f * TILE : (f + 1) * TILE, :] = jnp.log(deg[0, f * slots + mine]) * LOG10E
        degree_freq[f * TILE : (f + 1) * TILE, :] = freq[:, :BINS]
        diagonal = lane == sublane + f * TILE
        slope_row += jnp.sum(jnp.where(diagonal, slope, 0.0), axis=0, keepdims=True)
        mean_row += jnp.sum(jnp.where(diagonal, mean, 0.0), axis=0, keepdims=True)

    if rest:
        base = slots * full
        row_power = [(sublane + t * TILE) // slots for t in range(tail)]
        row_slot = [(sublane + t * TILE) % slots for t in range(tail)]

        def per_power(columns, combine, neutral):
            whole = [zero for _ in range(tail)]
            for q in range(rest):
                picked = [
                    jnp.where(row_power[t] == q, columns[t], neutral) for t in range(tail)
                ]
                merged = functools.reduce(combine, picked)
                reduce = jnp.max if combine is jnp.maximum else jnp.sum
                value = reduce(merged, axis=0, keepdims=True)
                whole = [jnp.where(row_power[t] == q, value, whole[t]) for t in range(tail)]
            return whole

        tops, totals, counts = [], [], []
        for t in range(tail):
            top = deg[0, base + t]
            for g in range(groups):
                top = jnp.maximum(top, deg[g, base + t])
            tops.append(jnp.max(top, axis=1, keepdims=True))
        peaks = per_power(tops, jnp.maximum, 0.0)
        for t in range(tail):
            inverse = 1.0 / peaks[t]
            total, count = zero, [zero] * BINS
            for g in range(groups):
                value = deg[g ^ start, base + t]
                total = total + value
                count = hat(value, inverse, count)
            totals.append(jnp.sum(total, axis=1, keepdims=True))
            counts.append([jnp.sum(c, axis=1, keepdims=True) for c in count])
        totals = per_power(totals, jnp.add, 0.0)
        freqs = per_power([on_lanes(c) for c in counts], jnp.add, 0.0)
        for q in range(rest):
            t, r = q * slots // TILE, q * slots % TILE
            p = full * TILE + q
            slope, mean = line(peaks[t], freqs[t], totals[t])
            degree_freq[p : p + 1, :] = freqs[t][r : r + 1, :BINS]
            here = (lane == p) & (sublane == r)
            slope_row += jnp.sum(jnp.where(here, slope, 0.0), axis=0, keepdims=True)
            mean_row += jnp.sum(jnp.where(here, mean, 0.0), axis=0, keepdims=True)
            own = zero
            for t in range(tail):
                hit = (row_power[t] == q) & (row_slot[t] == mine)
                own = own + jnp.where(hit, deg[0, base + t], 0.0)
            log_degree[p : p + 1, :] = jnp.log(jnp.sum(own, axis=0, keepdims=True)) * LOG10E
    fit_slope[...] = slope_row[:, :npower]
    mean_log[...] = mean_row[:, :npower]


def fit(npower, slots, place, deg):
    genes = deg.shape[-1]
    return pl.pallas_call(
        functools.partial(fit_kernel, npower, slots),
        out_shape=(
            jax.ShapeDtypeStruct((npower, genes), jnp.float32),
            jax.ShapeDtypeStruct((npower, BINS), jnp.float32),
            jax.ShapeDtypeStruct((1, npower), jnp.float32),
            jax.ShapeDtypeStruct((1, npower), jnp.float32),
        ),
        in_specs=[smem_spec(), vmem_spec()],
        out_specs=(vmem_spec(),) * 4,
        compiler_params=pltpu.CompilerParams(vmem_limit_bytes=VMEM_LIMIT),
    )(place, deg)


def bits_of(low, high):
    bits = []
    while low < high:
        bits.append(low)
        low *= 2
    return bits


def split_bits(rows, cols):
    devices = rows * cols
    col_bits, row_bits = bits_of(1, cols), bits_of(2 * cols, devices)
    far = col_bits[len(col_bits) // 2 :] + row_bits[len(row_bits) // 2 :]
    near = col_bits[: len(col_bits) // 2] + row_bits[: len(row_bits) // 2]
    return [bit ^ cols for bit in far], [bit ^ cols for bit in near]


def on_device(expression, powers):
    rows, cols = lax.axis_size("row"), lax.axis_size("col")
    devices = rows * cols
    npower = powers.shape[0]
    me = lax.axis_index(AXES)
    far, near = split_bits(rows, cols)
    core = cols

    def from_partner(array, bit):
        return lax.ppermute(array, AXES, [(i, i ^ bit) for i in range(devices)])

    def digit(bits, source):
        value = jnp.zeros((), jnp.int32)
        for i, bit in enumerate(bits):
            value = value | jnp.where(source & bit != 0, 1 << i, 0)
        return value

    parity = (me & core) // core
    for bit in far:
        parity = parity ^ jnp.where(me & (bit ^ core) != 0, 1, 0)
    for bit in near:
        parity = parity ^ jnp.where(me & (bit ^ core) != 0, 1, 0)
    mine = digit([bit ^ core for bit in far], me)
    start = digit([bit ^ core for bit in near], me) | parity << len(near)
    place = jnp.stack([mine, start]).astype(jnp.int32)

    lane_blocks = [expression]
    for bit in far:
        lane_blocks += [from_partner(block, bit) for block in lane_blocks]
    sub_blocks = [expression]
    for bit in near:
        sub_blocks += [from_partner(block, bit) for block in sub_blocks]
    sub_blocks += [from_partner(block, core) for block in sub_blocks]

    split = len(lane_blocks) - max(len(lane_blocks) // 4, 1)
    sub_stats = [stats(sub_blocks)]
    part = degrees(powers, lane_blocks[:split], sub_blocks, sub_stats)
    part = degrees(powers, lane_blocks[split:], sub_blocks, sub_stats, place, part)

    for bit in far:
        part = part + from_partner(part, bit)
    part = part[None]
    for bit in near + [core]:
        part = jnp.concatenate([part, from_partner(part, bit)])

    log_degree, degree_freq, fit_slope, mean_log = fit(
        npower, len(lane_blocks), place, part
    )
    return log_degree, degree_freq, fit_slope[0], mean_log[0]


def solution(mesh):
    return jax.shard_map(
        on_device,
        mesh=mesh,
        in_specs=(P(AXES, None), P()),
        out_specs=(P(None, AXES), P(), P(), P()),
        check_vma=False,
    )
```

time: 202 us -> 54.6 us (0.27)
  blocking collectives: 79.4 us -> 0 us
  waiting for transfers between devices: 77.6 us -> 26.6 us
  matrix products: 17.6 us -> 0 us
  starting transfers between devices: 0.11 us -> 17.2 us
  between operations: 13.8 us -> 0.7 us
  other arithmetic: 10.3 us -> 0.11 us
  Pallas kernels: 0 us -> 8.87 us
    all_gather x2 -> x0, waiting for transfers between devices: 56.9 us -> none  [the longest x1 30.9 us: on_device(): left_genes = lax.all_gather(expression, 'col', axis=0, tiled=True)]
    psum x1 -> x0, blocking collectives: 40.9 us -> none  [on_device(): lax.psum((jnp.sum(weights, axis=1), jnp.sum(degree, axis=1)), ('row', 'co...]
    pmax x1 -> x0, blocking collectives: 38.4 us -> none  [on_device(): peak = lax.pmax(jnp.max(degree, axis=1), ('row', 'col'))]
    ppermute x0 -> x15, waiting for transfers between devices: none -> 26.6 us  [from_partner(): return lax.ppermute(array, AXES, [(i, i ^ bit) for i in range(devices)])]
    reduce_scatter x1 -> x0, waiting for transfers between devices: 19.3 us -> none  [on_device(): lax.psum_scatter(row_totals, 'col', scatter_dimension=1, tiled=True)]
    dot_general x2 -> x0, matrix products: 17.6 us -> none  [one_block(): lax.dot_general(row_block, right_genes, (((1,), (1,)), ((), ())), preferr...]
    ppermute x0 -> x15, starting transfers between devices: none -> 17.2 us  [from_partner(): return lax.ppermute(array, AXES, [(i, i ^ bit) for i in range(devices)])]
    pallas_call x0 -> x4, Pallas kernels: none -> 8.87 us  [the longest x2 6.07 us: degrees(): pl.pallas_call(functools.partial(kernel, lane_count, sub_count, sizes), o...]
  transfers between devices with their start and end apart: 3 -> 15, of which waited for: 3 -> 9; matrix products, arithmetic and copies ran while one was open for 2% -> 0% of each run, Pallas kernels for 0% -> 10%
where the time goes in v1:
time: 54.6 us; the launch traced here: 54.4 us
  waiting for transfers between devices  26.6 us (49%)
  starting transfers between devices  17.2 us (32%)
  Pallas kernels  8.87 us (16%)
  local copies, waits for them, and re-layouts  0.95 us (2%)
  between operations  0.7 us (1%)
    ppermute x15, waiting for transfers between devices, from_partner(): return lax.ppermute(array, AXES, [(i, i ^ bit) for i in range(devices)])  26.6 us
    ppermute x15, starting transfers between devices, from_partner(): return lax.ppermute(array, AXES, [(i, i ^ bit) for i in range(devices)])  17.2 us
    pallas_call x2, Pallas kernels, degrees(): pl.pallas_call(functools.partial(kernel, lane_count, sub_count, sizes), o...  6.07 us
    pallas_call x1, Pallas kernels, fit(): pl.pallas_call(functools.partial(fit_kernel, npower, slots), out_shape=(j...  1.73 us
  transfers between devices with their start and end apart: 15, of which 9 were waited for; matrix products, arithmetic and copies ran while one was open for 0% of the time, Pallas kernels for 10%

profile of v1, /device:TPU:0, one launch (start us, length us, event | category | flops | bytes accessed | tf_op | source)
XLA Modules:
  0.0 54.4 jit_solution(7309085837810610996)
XLA Ops:
  0.6 2.6 %collective-permute-start.2 = (bf16[128,1024]{1,0:T(8,128)(2,1)}, bf16[128,1024]{1,0:T(8,128)(2,1)S(1)}, u32[]{:S(2)}, u32[]{:S(2)}) collective-permute-start(bf16[128,1024]{1,0:T(8,128)(2,1)} %refs_3_.1), channel_id=1, source_target_pairs={{0,5},{1,4},{2,7},{3,6},{4,1},{5,0},{6,3},{7,2},{8,13},{9,12},{10,... | collective-permute-start | bytes 786440 | tf_op jit(solution)/shard_map/ppermute | solution.py:332
  3.2 1.8 %collective-permute-start.3 = (bf16[128,1024]{1,0:T(8,128)(2,1)}, bf16[128,1024]{1,0:T(8,128)(2,1)S(1)}, u32[]{:S(2)}, u32[]{:S(2)}) collective-permute-start(bf16[128,1024]{1,0:T(8,128)(2,1)} %refs_3_.1), channel_id=1, source_target_pairs={{0,12},{1,13},{2,14},{3,15},{4,8},{5,9},{6,10},{7,11},{8,4},{9,5},... | collective-permute-start | bytes 786440 | tf_op jit(solution)/shard_map/ppermute | solution.py:332
  5.0 5.2 %collective-permute-done.2.refs_1_.refs_5_.refs_4_ = bf16[128,1024]{1,0:T(8,128)(2,1)S(1)} collective-permute-done((bf16[128,1024]{1,0:T(8,128)(2,1)}, bf16[128,1024]{1,0:T(8,128)(2,1)S(1)}, u32[]{:S(2)}, u32[]{:S(2)}) %collective-permute-start.2) | collective-permute-done | bytes 262176 | tf_op jit(solution)/shard_map/ppermute | solution.py:332
  10.2 2.0 %collective-permute-start.4 = (bf16[128,1024]{1,0:T(8,128)(2,1)S(1)}, bf16[128,1024]{1,0:T(8,128)(2,1)S(1)}, u32[]{:S(2)}, u32[]{:S(2)}) collective-permute-start(bf16[128,1024]{1,0:T(8,128)(2,1)S(1)} %collective-permute-done.2.refs_1_.refs_5_.refs_4_), channel_id=1, source_target_pairs={{0,12},{1,13},{2,14},{3,15},{4,8},{5,9},{6,10},{7,11},{8,4},{9,5},... | collective-permute-start | bytes 786440 | tf_op jit(solution)/shard_map/ppermute | solution.py:332
  12.2 0.3 collective-permute-start.5
  12.5 2.4 %collective-permute-start = (bf16[128,1024]{1,0:T(8,128)(2,1)}, bf16[128,1024]{1,0:T(8,128)(2,1)S(1)}, u32[]{:S(2)}, u32[]{:S(2)}) collective-permute-start(bf16[128,1024]{1,0:T(8,128)(2,1)} %refs_3_.1), channel_id=1, source_target_pairs={{0,6},{1,7},{2,4},{3,5},{4,2},{5,3},{6,0},{7,1},{8,14},{9,15},{10,... | collective-permute-start | bytes 786440 | tf_op jit(solution)/shard_map/ppermute | solution.py:332
  14.9 0.3 collective-permute-start.6
  15.2 0.0 collective-permute-done.3.refs_2_.refs_6_.refs_5_
  15.2 0.3 collective-permute-start.7
  15.4 3.2 %collective-permute-done.4.refs_3_.refs_7_.refs_6_ = bf16[128,1024]{1,0:T(8,128)(2,1)S(1)} collective-permute-done((bf16[128,1024]{1,0:T(8,128)(2,1)S(1)}, bf16[128,1024]{1,0:T(8,128)(2,1)S(1)}, u32[]{:S(2)}, u32[]{:S(2)}) %collective-permute-start.4) | collective-permute-done | bytes 262176 | tf_op jit(solution)/shard_map/ppermute | solution.py:332
  18.6 0.6 %collective-permute-start.8 = (bf16[128,1024]{1,0:T(8,128)(2,1)S(1)}, bf16[128,1024]{1,0:T(8,128)(2,1)S(1)}, u32[]{:S(2)}, u32[]{:S(2)}) collective-permute-start(bf16[128,1024]{1,0:T(8,128)(2,1)S(1)} %collective-permute-done.4.refs_3_.refs_7_.refs_6_), channel_id=1, source_target_pairs={{0,4},{1,5},{2,6},{3,7},{4,0},{5,1},{6,2},{7,3},{8,12},{9,13},{10,... | collective-permute-start | bytes 786440 | tf_op jit(solution)/shard_map/ppermute | solution.py:332
  19.2 0.0 collective-permute-done.5.refs_4_.refs_8_.refs_7_
  19.2 1.5 %collective-permute-start.9 = (bf16[128,1024]{1,0:T(8,128)(2,1)}, bf16[128,1024]{1,0:T(8,128)(2,1)S(1)}, u32[]{:S(2)}, u32[]{:S(2)}) collective-permute-start(bf16[128,1024]{1,0:T(8,128)(2,1)} %refs_3_.1), channel_id=1, source_target_pairs={{0,20},{1,21},{2,22},{3,23},{4,16},{5,17},{6,18},{7,19},{8,28},{9,... | collective-permute-start | bytes 786440 | tf_op jit(solution)/shard_map/ppermute | solution.py:332
  20.7 6.7 %collective-permute-done.refs_2_ = bf16[128,1024]{1,0:T(8,128)(2,1)S(1)} collective-permute-done((bf16[128,1024]{1,0:T(8,128)(2,1)}, bf16[128,1024]{1,0:T(8,128)(2,1)S(1)}, u32[]{:S(2)}, u32[]{:S(2)}) %collective-permute-start) | collective-permute-done | bytes 262176 | tf_op jit(solution)/shard_map/ppermute | solution.py:332
  27.4 1.4 %collective-permute-start.1 = (bf16[128,1024]{1,0:T(8,128)(2,1)S(1)}, bf16[128,1024]{1,0:T(8,128)(2,1)S(1)}, u32[]{:S(2)}, u32[]{:S(2)}) collective-permute-start(bf16[128,1024]{1,0:T(8,128)(2,1)S(1)} %collective-permute-done.refs_2_), channel_id=1, source_target_pairs={{0,20},{1,21},{2,22},{3,23},{4,16},{5,17},{6,18},{7,19},{8,28},{9,... | collective-permute-start | bytes 786440 | tf_op jit(solution)/shard_map/ppermute | solution.py:332
  28.7 0.0 copy-start.1
  28.7 0.1 pad_add_fusion.refs_1_.place
  28.8 0.0 collective-permute-done.6.refs_5_.refs_9_.refs_8_
  28.8 0.0 collective-permute-done.7.refs_6_.refs_10_.refs_9_
  28.8 0.0 collective-permute-done.8.refs_7_.refs_11_.refs_10_
  28.8 0.0 copy-start
  28.8 0.9 %copy-done = bf16[128,1024]{1,0:T(8,128)(2,1)S(1)} copy-done((bf16[128,1024]{1,0:T(8,128)(2,1)S(1)}, bf16[128,1024]{1,0:T(8,128)(2,1)}, u32[]{:S(2)}) %copy-start) | copy-done | bytes 262168
  29.8 1.1 %shard_map.57.refs_12_.refs_11_ = f32[8,2,128,128]{3,2,1,0:T(8,128)S(1)} custom-call(bf16[128,1024]{1,0:T(8,128)(2,1)S(1)} %copy-done, bf16[128,1024]{1,0:T(8,128)(2,1)S(1)} %collective-permute-done.2.refs_1_.refs_5_.refs_4_, bf16[128,1024]{1,0:T(8,128)(2,1)S(1)} %collective-permute-done.3.refs_2_.refs_6_.refs_5_, ...), custom_call_target="tpu_custom_call" | custom-call | flops 3200000 | bytes 3200000 | tf_op jit(solution)/shard_map/pallas_call | solution.py:52
  30.9 0.0 collective-permute-done.9.refs_3_
  30.9 0.0 copy-done.1
  30.9 4.2 %shard_map.58.refs_12_ = f32[3,10,128]{2,1,0:T(8,128)S(1)} custom-call(s32[10]{0:T(128)S(1)} %copy-done.1, bf16[128,1024]{1,0:T(8,128)(2,1)S(1)} %copy-done, bf16[128,1024]{1,0:T(8,128)(2,1)S(1)} %collective-permute-done.refs_2_, bf16[128,1024]{1,0:T(8,128)(2,1)S(1)} %collective-permute-done.9.refs_3_, bf16[128,1024]{1,0:T(8,128)(2,1)S(1)} %copy-done, ...), custom_call_target="tpu_custom_call" | custom-call | flops 805306368 | bytes 2883584 | tf_op jit(solution)/shard_map/pallas_call | solution.py:167
  35.1 0.4 collective-permute-done.1.refs_2_
  35.5 1.8 %shard_map.59 = f32[5,8,128]{2,1,0:T(8,128)S(1)} custom-call(s32[10]{0:T(128)S(1)} %copy-done.1, s32[2]{0:T(128)S(1)} %pad_add_fusion.refs_1_.place, bf16[128,1024]{1,0:T(8,128)(2,1)S(1)} %collective-permute-done.1.refs_2_, bf16[128,1024]{1,0:T(8,128)(2,1)S(1)} %copy-done, bf16[128,1024]{1,0:T(8,128)(2,1)S(1)} %collective-permute-done.2.refs_1_.refs_5_.refs_4_, ...), custom_call_target="tpu_custom_call" | custom-call | flops 268435456 | bytes 2359296 | tf_op jit(solution)/shard_map/pallas_call | solution.py:167
  37.4 0.7 %collective-permute-start.10 = (f32[5,8,128]{2,1,0:T(8,128)S(1)}, f32[5,8,128]{2,1,0:T(8,128)S(1)}, u32[]{:S(2)}, u32[]{:S(2)}) collective-permute-start(f32[5,8,128]{2,1,0:T(8,128)S(1)} %shard_map.59), channel_id=1, source_target_pairs={{0,6},{1,7},{2,4},{3,5},{4,2},{5,3},{6,0},{7,1},{8,14},{9,15},{10,... | collective-permute-start | bytes 61448 | tf_op jit(solution)/shard_map/ppermute | solution.py:332
  38.0 3.5 %collective-permute-done.10 = f32[5,8,128]{2,1,0:T(8,128)S(1)} collective-permute-done((f32[5,8,128]{2,1,0:T(8,128)S(1)}, f32[5,8,128]{2,1,0:T(8,128)S(1)}, u32[]{:S(2)}, u32[]{:S(2)}) %collective-permute-start.10) | collective-permute-done | bytes 20512 | tf_op jit(solution)/shard_map/ppermute | solution.py:332
  41.5 1.4 %collective-permute-start.11 = (f32[5,8,128]{2,1,0:T(8,128)S(1)}, f32[5,8,128]{2,1,0:T(8,128)S(1)}, u32[]{:S(2)}, u32[]{:S(2)}) collective-permute-start(f32[5,8,128]{2,1,0:T(8,128)S(1)} %add.11), channel_id=1, source_target_pairs={{0,20},{1,21},{2,22},{3,23},{4,16},{5,17},{6,18},{7,19},{8,28},{9,... | collective-permute-start | bytes 61448 | tf_op jit(solution)/shard_map/ppermute | solution.py:332
  42.9 1.8 %collective-permute-done.11 = f32[5,8,128]{2,1,0:T(8,128)S(1)} collective-permute-done((f32[5,8,128]{2,1,0:T(8,128)S(1)}, f32[5,8,128]{2,1,0:T(8,128)S(1)}, u32[]{:S(2)}, u32[]{:S(2)}) %collective-permute-start.11) | collective-permute-done | bytes 20512 | tf_op jit(solution)/shard_map/ppermute | solution.py:332
  44.8 1.7 %collective-permute-start.12 = (f32[1,5,8,128]{3,2,1,0:T(8,128)S(1)}, f32[1,5,8,128]{3,2,1,0:T(8,128)S(1)}, u32[]{:S(2)}, u32[]{:S(2)}) collective-permute-start(f32[1,5,8,128]{3,2,1,0:T(8,128)S(1)} %add_bitcast_fusion), channel_id=1, source_target_pairs={{0,5},{1,4},{2,7},{3,6},{4,1},{5,0},{6,3},{7,2},{8,13},{9,12},{10,... | collective-permute-start | bytes 61448 | tf_op jit(solution)/shard_map/ppermute | solution.py:332
  46.4 1.5 %collective-permute-done.12 = f32[1,5,8,128]{3,2,1,0:T(8,128)S(1)} collective-permute-done((f32[1,5,8,128]{3,2,1,0:T(8,128)S(1)}, f32[1,5,8,128]{3,2,1,0:T(8,128)S(1)}, u32[]{:S(2)}, u32[]{:S(2)}) %collective-permute-start.12) | collective-permute-done | bytes 20512 | tf_op jit(solution)/shard_map/ppermute | solution.py:332
  48.0 0.2 collective-permute-start.13
  48.2 3.2 %collective-permute-done.13 = f32[2,5,8,128]{3,2,1,0:T(8,128)S(1)} collective-permute-done((f32[2,5,8,128]{3,2,1,0:T(8,128)S(1)}, f32[2,5,8,128]{3,2,1,0:T(8,128)S(1)}, u32[]{:S(2)}, u32[]{:S(2)}) %collective-permute-start.13) | collective-permute-done | bytes 40992 | tf_op jit(solution)/shard_map/ppermute | solution.py:332
  51.4 0.3 collective-permute-start.14
  51.7 1.0 %collective-permute-done.14 = f32[4,5,8,128]{3,2,1,0:T(8,128)S(1)} collective-permute-done((f32[4,5,8,128]{3,2,1,0:T(8,128)S(1)}, f32[4,5,8,128]{3,2,1,0:T(8,128)S(1)}, u32[]{:S(2)}, u32[]{:S(2)}) %collective-permute-start.14) | collective-permute-done | bytes 81952 | tf_op jit(solution)/shard_map/ppermute | solution.py:332
  52.7 1.7 %shard_map.60 = (f32[10,128]{1,0:T(8,128)}, f32[10,10]{1,0:T(8,128)}, f32[1,10]{1,0:T(1,128)}, f32[1,10]{1,0:T(1,128)}) custom-call(s32[2]{0:T(128)S(1)} %pad_add_fusion.refs_1_.place, f32[8,5,8,128]{3,2,1,0:T(8,128)S(1)} %pad_maximum_fusion.deg), custom_call_target="tpu_custom_call" | custom-call | tf_op jit(solution)/shard_map/pallas_call | solution.py:293
  (5 shorter events, 0.0 us)
Async XLA Ops:
  0.6 9.6 %collective-permute-start.2 = (bf16[128,1024]{1,0:T(8,128)(2,1)}, bf16[128,1024]{1,0:T(8,128)(2,1)S(1)}, u32[]{:S(2)}, u32[]{:S(2)}) collective-permute-start(bf16[128,1024]{1,0:T(8,128)(2,1)} %refs_3_.1), channel_id=1, source_target_pairs={{0,5},{1,4},{2,7},{3,6},{4,1},{5,0},{6,3},{7,2},{8,13},{9,12},{10,... | collective-permute-start | bytes 786440 | tf_op jit(solution)/shard_map/ppermute | solution.py:332
  3.2 12.0 %collective-permute-start.3 = (bf16[128,1024]{1,0:T(8,128)(2,1)}, bf16[128,1024]{1,0:T(8,128)(2,1)S(1)}, u32[]{:S(2)}, u32[]{:S(2)}) collective-permute-start(bf16[128,1024]{1,0:T(8,128)(2,1)} %refs_3_.1), channel_id=1, source_target_pairs={{0,12},{1,13},{2,14},{3,15},{4,8},{5,9},{6,10},{7,11},{8,4},{9,5},... | collective-permute-start | bytes 786440 | tf_op jit(solution)/shard_map/ppermute | solution.py:332
  10.2 8.4 %collective-permute-start.4 = (bf16[128,1024]{1,0:T(8,128)(2,1)S(1)}, bf16[128,1024]{1,0:T(8,128)(2,1)S(1)}, u32[]{:S(2)}, u32[]{:S(2)}) collective-permute-start(bf16[128,1024]{1,0:T(8,128)(2,1)S(1)} %collective-permute-done.2.refs_1_.refs_5_.refs_4_), channel_id=1, source_target_pairs={{0,12},{1,13},{2,14},{3,15},{4,8},{5,9},{6,10},{7,11},{8,4},{9,5},... | collective-permute-start | bytes 786440 | tf_op jit(solution)/shard_map/ppermute | solution.py:332
  12.2 7.0 %collective-permute-start.5 = (bf16[128,1024]{1,0:T(8,128)(2,1)}, bf16[128,1024]{1,0:T(8,128)(2,1)S(1)}, u32[]{:S(2)}, u32[]{:S(2)}) collective-permute-start(bf16[128,1024]{1,0:T(8,128)(2,1)} %refs_3_.1), channel_id=1, source_target_pairs={{0,4},{1,5},{2,6},{3,7},{4,0},{5,1},{6,2},{7,3},{8,12},{9,13},{10,... | collective-permute-start | bytes 786440 | tf_op jit(solution)/shard_map/ppermute | solution.py:332
  12.5 14.9 %collective-permute-start = (bf16[128,1024]{1,0:T(8,128)(2,1)}, bf16[128,1024]{1,0:T(8,128)(2,1)S(1)}, u32[]{:S(2)}, u32[]{:S(2)}) collective-permute-start(bf16[128,1024]{1,0:T(8,128)(2,1)} %refs_3_.1), channel_id=1, source_target_pairs={{0,6},{1,7},{2,4},{3,5},{4,2},{5,3},{6,0},{7,1},{8,14},{9,15},{10,... | collective-permute-start | bytes 786440 | tf_op jit(solution)/shard_map/ppermute | solution.py:332
  14.9 13.9 %collective-permute-start.6 = (bf16[128,1024]{1,0:T(8,128)(2,1)S(1)}, bf16[128,1024]{1,0:T(8,128)(2,1)S(1)}, u32[]{:S(2)}, u32[]{:S(2)}) collective-permute-start(bf16[128,1024]{1,0:T(8,128)(2,1)S(1)} %collective-permute-done.2.refs_1_.refs_5_.refs_4_), channel_id=1, source_target_pairs={{0,4},{1,5},{2,6},{3,7},{4,0},{5,1},{6,2},{7,3},{8,12},{9,13},{10,... | collective-permute-start | bytes 786440 | tf_op jit(solution)/shard_map/ppermute | solution.py:332
  15.2 13.7 %collective-permute-start.7 = (bf16[128,1024]{1,0:T(8,128)(2,1)S(1)}, bf16[128,1024]{1,0:T(8,128)(2,1)S(1)}, u32[]{:S(2)}, u32[]{:S(2)}) collective-permute-start(bf16[128,1024]{1,0:T(8,128)(2,1)S(1)} %collective-permute-done.3.refs_2_.refs_6_.refs_5_), channel_id=1, source_target_pairs={{0,4},{1,5},{2,6},{3,7},{4,0},{5,1},{6,2},{7,3},{8,12},{9,13},{10,... | collective-permute-start | bytes 786440 | tf_op jit(solution)/shard_map/ppermute | solution.py:332
  18.6 10.2 %collective-permute-start.8 = (bf16[128,1024]{1,0:T(8,128)(2,1)S(1)}, bf16[128,1024]{1,0:T(8,128)(2,1)S(1)}, u32[]{:S(2)}, u32[]{:S(2)}) collective-permute-start(bf16[128,1024]{1,0:T(8,128)(2,1)S(1)} %collective-permute-done.4.refs_3_.refs_7_.refs_6_), channel_id=1, source_target_pairs={{0,4},{1,5},{2,6},{3,7},{4,0},{5,1},{6,2},{7,3},{8,12},{9,13},{10,... | collective-permute-start | bytes 786440 | tf_op jit(solution)/shard_map/ppermute | solution.py:332
  19.2 11.7 %collective-permute-start.9 = (bf16[128,1024]{1,0:T(8,128)(2,1)}, bf16[128,1024]{1,0:T(8,128)(2,1)S(1)}, u32[]{:S(2)}, u32[]{:S(2)}) collective-permute-start(bf16[128,1024]{1,0:T(8,128)(2,1)} %refs_3_.1), channel_id=1, source_target_pairs={{0,20},{1,21},{2,22},{3,23},{4,16},{5,17},{6,18},{7,19},{8,28},{9,... | collective-permute-start | bytes 786440 | tf_op jit(solution)/shard_map/ppermute | solution.py:332
  27.4 8.2 %collective-permute-start.1 = (bf16[128,1024]{1,0:T(8,128)(2,1)S(1)}, bf16[128,1024]{1,0:T(8,128)(2,1)S(1)}, u32[]{:S(2)}, u32[]{:S(2)}) collective-permute-start(bf16[128,1024]{1,0:T(8,128)(2,1)S(1)} %collective-permute-done.refs_2_), channel_id=1, source_target_pairs={{0,20},{1,21},{2,22},{3,23},{4,16},{5,17},{6,18},{7,19},{8,28},{9,... | collective-permute-start | bytes 786440 | tf_op jit(solution)/shard_map/ppermute | solution.py:332
  28.7 2.1 %copy-start.1 = (s32[10]{0:T(128)S(1)}, s32[10]{0:T(128)}, u32[]{:S(2)}) copy-start(s32[10]{0:T(128)} %refs_0_.5) | copy-start | bytes 124
  28.8 1.0 %copy-start = (bf16[128,1024]{1,0:T(8,128)(2,1)S(1)}, bf16[128,1024]{1,0:T(8,128)(2,1)}, u32[]{:S(2)}) copy-start(bf16[128,1024]{1,0:T(8,128)(2,1)} %refs_3_.1) | copy-start | bytes 786436
  37.4 4.2 %collective-permute-start.10 = (f32[5,8,128]{2,1,0:T(8,128)S(1)}, f32[5,8,128]{2,1,0:T(8,128)S(1)}, u32[]{:S(2)}, u32[]{:S(2)}) collective-permute-start(f32[5,8,128]{2,1,0:T(8,128)S(1)} %shard_map.59), channel_id=1, source_target_pairs={{0,6},{1,7},{2,4},{3,5},{4,2},{5,3},{6,0},{7,1},{8,14},{9,15},{10,... | collective-permute-start | bytes 61448 | tf_op jit(solution)/shard_map/ppermute | solution.py:332
  41.5 3.2 %collective-permute-start.11 = (f32[5,8,128]{2,1,0:T(8,128)S(1)}, f32[5,8,128]{2,1,0:T(8,128)S(1)}, u32[]{:S(2)}, u32[]{:S(2)}) collective-permute-start(f32[5,8,128]{2,1,0:T(8,128)S(1)} %add.11), channel_id=1, source_target_pairs={{0,20},{1,21},{2,22},{3,23},{4,16},{5,17},{6,18},{7,19},{8,28},{9,... | collective-permute-start | bytes 61448 | tf_op jit(solution)/shard_map/ppermute | solution.py:332
  44.8 3.2 %collective-permute-start.12 = (f32[1,5,8,128]{3,2,1,0:T(8,128)S(1)}, f32[1,5,8,128]{3,2,1,0:T(8,128)S(1)}, u32[]{:S(2)}, u32[]{:S(2)}) collective-permute-start(f32[1,5,8,128]{3,2,1,0:T(8,128)S(1)} %add_bitcast_fusion), channel_id=1, source_target_pairs={{0,5},{1,4},{2,7},{3,6},{4,1},{5,0},{6,3},{7,2},{8,13},{9,12},{10,... | collective-permute-start | bytes 61448 | tf_op jit(solution)/shard_map/ppermute | solution.py:332
  48.0 3.4 %collective-permute-start.13 = (f32[2,5,8,128]{3,2,1,0:T(8,128)S(1)}, f32[2,5,8,128]{3,2,1,0:T(8,128)S(1)}, u32[]{:S(2)}, u32[]{:S(2)}) collective-permute-start(f32[2,5,8,128]{3,2,1,0:T(8,128)S(1)} %pad_maximum_fusion.2), channel_id=1, source_target_pairs={{0,12},{1,13},{2,14},{3,15},{4,8},{5,9},{6,10},{7,11},{8,4},{9,5},... | collective-permute-start | bytes 122888 | tf_op jit(solution)/shard_map/ppermute | solution.py:332
  51.4 1.3 %collective-permute-start.14 = (f32[4,5,8,128]{3,2,1,0:T(8,128)S(1)}, f32[4,5,8,128]{3,2,1,0:T(8,128)S(1)}, u32[]{:S(2)}, u32[]{:S(2)}) collective-permute-start(f32[4,5,8,128]{3,2,1,0:T(8,128)S(1)} %pad_maximum_fusion.1), channel_id=1, source_target_pairs={{0,4},{1,5},{2,6},{3,7},{4,0},{5,1},{6,2},{7,3},{8,12},{9,13},{10,... | collective-permute-start | bytes 245768 | tf_op jit(solution)/shard_map/ppermute | solution.py:332

commit v2 on v1

v2 whole, which is shorter than its diff:
```python
import functools

import jax
import jax.numpy as jnp
from jax import lax
from jax.experimental import pallas as pl
from jax.experimental.pallas import tpu as pltpu
from jax.sharding import PartitionSpec as P


BINS = 10
AXES = ("row", "col")
LOG2E = 1.4426950408889634
LOG10E = 0.4342944819032518
TILE = 8
CHUNK = 32
PIECES = 2
VMEM_LIMIT = 20 * 2**20


def gene_stats(genes):
    values = genes.astype(jnp.float32)
    samples = values.shape[1]
    mean = jnp.sum(values, axis=1, keepdims=True) * (1.0 / samples)
    centred = values - mean
    var = jnp.sum(centred * centred, axis=1, keepdims=True) * (1.0 / samples)
    return mean, lax.rsqrt(var + 1e-06)


def as_row(column):
    genes = column.shape[0]
    return jnp.transpose(jnp.broadcast_to(column, (genes, genes)))[0:1, :]


def vmem_spec():
    return pl.BlockSpec(memory_space=pltpu.VMEM)


def pallas(kernel, out_shape, operands, scratch=(), cost=None):
    return pl.pallas_call(
        kernel,
        out_shape=out_shape,
        in_specs=[vmem_spec()] * len(operands),
        out_specs=jax.tree.map(lambda _: vmem_spec(), out_shape),
        scratch_shapes=list(scratch),
        compiler_params=pltpu.CompilerParams(vmem_limit_bytes=VMEM_LIMIT),
        cost_estimate=cost,
    )(*operands)


def f32(*shape):
    return jax.ShapeDtypeStruct(shape, jnp.float32)


def split_refs(refs, sizes):
    groups = []
    for size in sizes:
        groups.append(refs[:size])
        refs = refs[size:]
    return groups, refs


def whole(parts):
    return jnp.concatenate([part[...] for part in parts], axis=1)


def measure_sub(block, out):
    genes, samples = block.shape
    mean, inv = gene_stats(block)
    out[0] = jnp.broadcast_to(mean * samples, (genes, genes))
    out[1] = jnp.broadcast_to(inv * (1.0 / samples), (genes, genes))


def row_sums(raw, column, sub_stats, lane_mean, lane_inv, scales):
    npower, _, genes = scales.shape
    sums = [jnp.zeros((TILE, genes), jnp.float32) for _ in range(npower)]
    for b, stat in enumerate(sub_stats):
        for c in range(0, genes, CHUNK):
            part = slice(c, c + CHUNK)
            pearson = (
                (raw[b, part, column] - stat[0, part, :] * lane_mean)
                * stat[1, part, :]
                * lane_inv
            )
            log_abs = jnp.log(jnp.abs(pearson)).reshape(CHUNK // TILE, TILE, genes)
            for p in range(npower):
                term = jnp.exp2(log_abs * scales[p])
                sums[p] = sums[p] + jnp.sum(term, axis=0)
    return [jnp.sum(total, axis=0, keepdims=True) for total in sums]


def multiply(raw, sub_refs, lanes):
    for b, sub_ref in enumerate(sub_refs):
        raw[b] = lax.dot_general(
            sub_ref[...], lanes, (((1,), (1,)), ((), ())), preferred_element_type=jnp.float32
        )


def early_kernel(lane_sizes, sub_count, scales, place, *refs):
    lanes, refs = split_refs(refs, lane_sizes)
    subs, (out, sub_stats, raw) = refs[:sub_count], refs[sub_count:]
    _, _, genes = scales.shape
    blocks = [whole(parts) for parts in lanes]
    multiply(raw, subs, jnp.concatenate(blocks, axis=0))
    for b, sub in enumerate(subs):
        measure_sub(sub[...], sub_stats.at[b])
    stat_refs = [sub_stats.at[b] for b in range(sub_count)]
    for a, block in enumerate(blocks):
        mean, inv = gene_stats(block)
        mean, inv = as_row(mean), as_row(inv)
        column = slice(a * genes, (a + 1) * genes)
        rows = row_sums(raw, column, stat_refs, mean, inv, scales)
        for p, row in enumerate(rows + [mean, inv]):
            out[a, p : p + 1, :] = row


def late_kernel(here_sizes, last_sizes, first_count, second_count, scales, place, *refs):
    here, refs = split_refs(refs, here_sizes)
    last, refs = split_refs(refs, last_sizes)
    (first, second), refs = split_refs(refs, (first_count, second_count))
    first_stats, prior, out, raw_here, raw_last, second_stats = refs
    npower, _, genes = scales.shape
    slots = len(here) + len(last)
    full, rest = npower // TILE, npower % TILE
    second_refs = [second_stats.at[b] for b in range(second_count)]
    all_refs = [first_stats.at[b] for b in range(first_count)] + second_refs
    rows = []
    multiply(raw_here, second, jnp.concatenate([whole(parts) for parts in here], axis=0))
    for b, sub in enumerate(second):
        measure_sub(sub[...], second_stats.at[b])
    blocks = [whole(parts) for parts in last]
    multiply(raw_last, first + second, jnp.concatenate(blocks, axis=0))
    for a in range(len(here)):
        mean, inv = prior[a, npower : npower + 1, :], prior[a, npower + 1 : npower + 2, :]
        column = slice(a * genes, (a + 1) * genes)
        added = row_sums(raw_here, column, second_refs, mean, inv, scales)
        rows.append([row + prior[a, p : p + 1, :] for p, row in enumerate(added)])
    for a, block in enumerate(blocks):
        mean, inv = gene_stats(block)
        column = slice(a * genes, (a + 1) * genes)
        rows.append(row_sums(raw_last, column, all_refs, as_row(mean), as_row(inv), scales))

    mine = place[...]
    sublane = lax.broadcasted_iota(jnp.int32, (TILE, genes), 0)
    for f in range(full):
        for target in range(slots):
            tile = jnp.concatenate(rows[0][f * TILE : (f + 1) * TILE], axis=0)
            for s in range(1, slots):
                other = jnp.concatenate(rows[s][f * TILE : (f + 1) * TILE], axis=0)
                tile = jnp.where(mine == (s ^ target), other, tile)
            out[f * slots + target] = tile
    for t in range(out.shape[0] - full * slots):
        tile = jnp.zeros((TILE, genes), jnp.float32)
        for q in range(rest):
            for s in range(slots):
                hit = sublane + t * TILE == q * slots + (mine ^ s)
                tile = jnp.where(hit, rows[s][full * TILE + q], tile)
        out[full * slots + t] = tile


def tile_count(npower, slots):
    return slots * (npower // TILE) + -(-(npower % TILE) * slots // TILE)


def work(pairs, samples, npower):
    return pl.CostEstimate(
        flops=2 * pairs * samples, bytes_accessed=4 * pairs, transcendentals=pairs * (npower + 1)
    )


def flat(blocks):
    return [part for parts in blocks for part in parts]


def sizes_of(blocks):
    return [len(parts) for parts in blocks]


def early_sums(scales, place, here, first):
    genes, samples = first[0].shape
    npower = scales.shape[0]
    return pallas(
        functools.partial(early_kernel, sizes_of(here), len(first)),
        (f32(len(here), npower + 2, genes), f32(len(first), 2, genes, genes)),
        [scales, place] + flat(here) + first,
        [pltpu.VMEM((len(first), genes, len(here) * genes), jnp.float32)],
        work(len(here) * len(first) * genes * genes, samples, npower),
    )


def late_sums(scales, place, here, last, first, second, first_stats, prior):
    genes, samples = first[0].shape
    npower = scales.shape[0]
    blocks = len(here) * len(second) + len(last) * (len(first) + len(second))
    return pallas(
        functools.partial(
            late_kernel, sizes_of(here), sizes_of(last), len(first), len(second)
        ),
        f32(tile_count(npower, len(here) + len(last)), TILE, genes),
        [scales, place] + flat(here) + flat(last) + first + second + [first_stats, prior],
        [
            pltpu.VMEM((len(second), genes, len(here) * genes), jnp.float32),
            pltpu.VMEM((len(first) + len(second), genes, len(last) * genes), jnp.float32),
            pltpu.VMEM((len(second), 2, genes, genes), jnp.float32),
        ],
        work(blocks * genes * genes, samples, npower),
    )


def fit_kernel(npower, slots, place, deg, own, log_degree, degree_freq, fit_slope, mean_log):
    groups, tiles, _, genes = deg.shape
    full, rest = npower // TILE, npower % TILE
    total_genes = groups * slots * genes
    inv_genes = 1.0 / total_genes
    mine = place[...]
    tail = tiles - slots * full
    sublane = lax.broadcasted_iota(jnp.int32, (TILE, genes), 0)
    lane = lax.broadcasted_iota(jnp.int32, (TILE, genes), 1)
    slope_row, mean_row = 0.0, 0.0

    def hat(value, inverse, counts):
        position = jnp.clip(BINS * value * inverse - 0.5, 0.0, BINS - 1.0)
        return [
            count + jnp.maximum(0.0, 1.0 - jnp.abs(position - b)) for b, count in enumerate(counts)
        ]

    def line(peak, freq, total):
        used = lane < BINS
        centre = lane.astype(jnp.float32) + 0.5
        xfit = jnp.where(used, jnp.log(centre * peak * (1.0 / BINS)) * LOG10E, 0.0)
        yfit = jnp.where(used, jnp.log(freq + inv_genes) * LOG10E, 0.0)
        xdev = jnp.where(used, xfit - jnp.sum(xfit, axis=1, keepdims=True) * (1.0 / BINS), 0.0)
        ydev = jnp.where(used, yfit - jnp.sum(yfit, axis=1, keepdims=True) * (1.0 / BINS), 0.0)
        slope = jnp.sum(xdev * ydev, axis=1, keepdims=True) / jnp.sum(
            xdev * xdev, axis=1, keepdims=True
        )
        return slope, jnp.log(total * inv_genes) * LOG10E

    def on_lanes(counts):
        freq = jnp.zeros((TILE, genes), jnp.float32)
        for b in range(BINS):
            freq = jnp.where(lane == b, counts[b] * inv_genes, freq)
        return freq

    zero = jnp.zeros((TILE, genes), jnp.float32)
    for f in range(full):
        top = deg[0, f * slots]
        for g in range(groups):
            for s in range(slots):
                top = jnp.maximum(top, deg[g, f * slots + s])
        peak = jnp.max(top, axis=1, keepdims=True)
        inverse = 1.0 / peak
        total, counts = zero, [zero] * BINS
        for g in range(groups):
            for s in range(slots):
                value = deg[g, f * slots + s]
                total = total + value
                counts = hat(value, inverse, counts)
        freq = on_lanes([jnp.sum(count, axis=1, keepdims=True) for count in counts])
        slope, mean = line(peak, freq, jnp.sum(total, axis=1, keepdims=True))
        value = own[f * slots]
        for s in range(1, slots):
            value = jnp.where(mine == s, own[f * slots + s], value)
        log_degree[f * TILE : (f + 1) * TILE, :] = jnp.log(value) * LOG10E
        degree_freq[f * TILE : (f + 1) * TILE, :] = freq[:, :BINS]
        diagonal = lane == sublane + f * TILE
        slope_row += jnp.sum(jnp.where(diagonal, slope, 0.0), axis=0, keepdims=True)
        mean_row += jnp.sum(jnp.where(diagonal, mean, 0.0), axis=0, keepdims=True)

    if rest:
        base = slots * full
        row_power = [(sublane + t * TILE) // slots for t in range(tail)]
        row_slot = [(sublane + t * TILE) % slots for t in range(tail)]

        def per_power(columns, combine, neutral):
            whole = [zero for _ in range(tail)]
            for q in range(rest):
                picked = [
                    jnp.where(row_power[t] == q, columns[t], neutral) for t in range(tail)
                ]
                merged = functools.reduce(combine, picked)
                reduce = jnp.max if combine is jnp.maximum else jnp.sum
                value = reduce(merged, axis=0, keepdims=True)
                whole = [jnp.where(row_power[t] == q, value, whole[t]) for t in range(tail)]
            return whole

        tops, totals, counts = [], [], []
        for t in range(tail):
            top = deg[0, base + t]
            for g in range(groups):
                top = jnp.maximum(top, deg[g, base + t])
            tops.append(jnp.max(top, axis=1, keepdims=True))
        peaks = per_power(tops, jnp.maximum, 0.0)
        for t in range(tail):
            inverse = 1.0 / peaks[t]
            total, count = zero, [zero] * BINS
            for g in range(groups):
                value = deg[g, base + t]
                total = total + value
                count = hat(value, inverse, count)
            totals.append(jnp.sum(total, axis=1, keepdims=True))
            counts.append([jnp.sum(c, axis=1, keepdims=True) for c in count])
        totals = per_power(totals, jnp.add, 0.0)
        freqs = per_power([on_lanes(c) for c in counts], jnp.add, 0.0)
        for q in range(rest):
            t, r = q * slots // TILE, q * slots % TILE
            p = full * TILE + q
            slope, mean = line(peaks[t], freqs[t], totals[t])
            degree_freq[p : p + 1, :] = freqs[t][r : r + 1, :BINS]
            here = (lane == p) & (sublane == r)
            slope_row += jnp.sum(jnp.where(here, slope, 0.0), axis=0, keepdims=True)
            mean_row += jnp.sum(jnp.where(here, mean, 0.0), axis=0, keepdims=True)
            value = zero
            for t in range(tail):
                hit = (row_power[t] == q) & (row_slot[t] == mine)
                value = value + jnp.where(hit, own[base + t], 0.0)
            log_degree[p : p + 1, :] = jnp.log(jnp.sum(value, axis=0, keepdims=True)) * LOG10E
    fit_slope[...] = slope_row[:, :npower]
    mean_log[...] = mean_row[:, :npower]


def fit(npower, slots, place, deg, own):
    genes = deg.shape[-1]
    return pallas(
        functools.partial(fit_kernel, npower, slots),
        (f32(npower, genes), f32(npower, BINS), f32(1, npower), f32(1, npower)),
        [place, deg, own],
    )


def bits_of(low, high):
    bits = []
    while low < high:
        bits.append(low)
        low *= 2
    return bits


def split_bits(rows, cols):
    devices = rows * cols
    col_bits, row_bits = bits_of(1, cols), bits_of(2 * cols, devices)
    far = col_bits[len(col_bits) // 2 :] + row_bits[len(row_bits) // 2 :]
    near = col_bits[: len(col_bits) // 2] + row_bits[: len(row_bits) // 2]
    return [bit ^ cols for bit in far], [bit ^ cols for bit in near]


def on_device(expression, powers):
    rows, cols = lax.axis_size("row"), lax.axis_size("col")
    devices = rows * cols
    npower = powers.shape[0]
    me = lax.axis_index(AXES)
    far, near = split_bits(rows, cols)
    core = cols

    def from_partner(array, bit):
        return lax.ppermute(array, AXES, [(i, i ^ bit) for i in range(devices)])

    mine = jnp.zeros((), jnp.int32)
    parity = me & core != 0
    for i, bit in enumerate(far):
        mine = mine | jnp.where(me & (bit ^ core) != 0, 1 << i, 0)
        parity = parity ^ (me & (bit ^ core) != 0)
    upper = []
    for bit in near:
        upper.append(me & (bit ^ core) != 0)
        parity = parity ^ upper[-1]
    upper.append(parity)
    genes, samples = expression.shape
    place = jnp.broadcast_to(mine, (TILE, genes))
    scales = jnp.broadcast_to(
        (powers.astype(jnp.float32) * LOG2E)[:, None, None], (npower, TILE, genes)
    )

    width = samples // PIECES
    pieces = tuple(expression[:, i * width : (i + 1) * width] for i in range(PIECES))
    lane_blocks = [(expression,)]
    for i, bit in enumerate(far):
        sent = [pieces] if i == 0 else lane_blocks
        lane_blocks = lane_blocks + [
            tuple(from_partner(part, bit) for part in parts)
            for parts in sent
        ]
    sub_blocks = [expression]
    for bit in near:
        sub_blocks += [from_partner(block, bit) for block in sub_blocks]
    crossed = [from_partner(block, core) for block in sub_blocks]

    quarter = max(len(lane_blocks) // 4, 1)
    here, last = lane_blocks[:-quarter], lane_blocks[-quarter:]
    quarter = max(len(sub_blocks) // 4, 1)
    first = sub_blocks[:-quarter] + crossed[:-quarter]
    second = sub_blocks[-quarter:] + crossed[-quarter:]
    part, first_stats = early_sums(scales, place, here, first)
    part = late_sums(scales, place, here, last, first, second, first_stats, part)

    for bit in far:
        part = part + from_partner(part, bit)
    own, part = part, part[None]
    for bit, up in zip(near + [core], upper):
        got = from_partner(part, bit)
        part = jnp.concatenate([jnp.where(up, got, part), jnp.where(up, part, got)])

    log_degree, degree_freq, fit_slope, mean_log = fit(npower, len(lane_blocks), place, part, own)
    return log_degree, degree_freq, fit_slope[0], mean_log[0]


def solution(mesh):
    return jax.shard_map(
        on_device,
        mesh=mesh,
        in_specs=(P(AXES, None), P()),
        out_specs=(P(None, AXES), P(), P(), P()),
        check_vma=False,
    )
```

time: 54.6 us -> 51.8 us (0.949)
  waiting for transfers between devices: 26.6 us -> 24.7 us
  Pallas kernels: 8.87 us -> 7.1 us
  starting transfers between devices: 17.2 us -> 17.9 us
    ppermute x15 -> x17, waiting for transfers between devices: 26.6 us -> 24.7 us  [from_partner(): return lax.ppermute(array, AXES, [(i, i ^ bit) for i in range(devices)])]
    pallas_call x4 -> x3, Pallas kernels: 8.87 us -> 7.1 us  [pallas(): pl.pallas_call(kernel, out_shape=out_shape, in_specs=[vmem_spec()] * len(...]
    slice x0 -> x1, local copies, waits for them, and re-layouts: none -> 0.99 us  [on_device(): expression[:, i * width:(i + 1) * width]]
    unnamed x4, local copies, waits for them, and re-layouts: 0.95 us -> 0.01 us
    ppermute x15 -> x17, starting transfers between devices: 17.2 us -> 17.9 us  [from_partner(): return lax.ppermute(array, AXES, [(i, i ^ bit) for i in range(devices)])]
  transfers between devices with their start and end apart: 15 -> 17, of which waited for: 9 -> 8; matrix products, arithmetic and copies ran while one was open for 0% -> 2% of each run, Pallas kernels for 10% -> 7%
where the time goes in v2:
time: 51.8 us; the launch traced here: 51.6 us
  waiting for transfers between devices  24.7 us (48%)
  starting transfers between devices  17.9 us (35%)
  Pallas kernels  7.1 us (14%)
  local copies, waits for them, and re-layouts  1.08 us (2%)
  between operations  0.74 us (1%)
    ppermute x17, waiting for transfers between devices, from_partner(): return lax.ppermute(array, AXES, [(i, i ^ bit) for i in range(devices)])  24.7 us
    ppermute x17, starting transfers between devices, from_partner(): return lax.ppermute(array, AXES, [(i, i ^ bit) for i in range(devices)])  17.9 us
    pallas_call x3, Pallas kernels, pallas(): pl.pallas_call(kernel, out_shape=out_shape, in_specs=[vmem_spec()] * len(...  7.1 us
  transfers between devices with their start and end apart: 17, of which 8 were waited for; matrix products, arithmetic and copies ran while one was open for 2% of the time, Pallas kernels for 7%

profile of v2, /device:TPU:0, one launch (start us, length us, event | category | flops | bytes accessed | tf_op | source)
XLA Modules:
  0.0 51.6 jit_solution(4437660368909491200)
XLA Ops:
  0.6 0.0 copy-start
  0.6 2.6 %collective-permute-start.5 = (bf16[128,1024]{1,0:T(8,128)(2,1)}, bf16[128,1024]{1,0:T(8,128)(2,1)S(1)}, u32[]{:S(2)}, u32[]{:S(2)}) collective-permute-start(bf16[128,1024]{1,0:T(8,128)(2,1)} %refs_6_.1), channel_id=1, source_target_pairs={{0,5},{1,4},{2,7},{3,6},{4,1},{5,0},{6,3},{7,2},{8,13},{9,12},{10,... | collective-permute-start | bytes 786440 | tf_op jit(solution)/shard_map/ppermute | solution.py:356
  3.2 1.0 %fusion = (bf16[128,512]{1,0:T(8,128)(2,1)S(1)}, bf16[128,512]{1,0:T(8,128)(2,1)S(1)}) fusion(bf16[128,1024]{1,0:T(8,128)(2,1)} %refs_6_.1), kind=kLoop, calls=%fused_computation.10 | loop fusion | bytes 524288 | tf_op jit(solution)/shard_map/slice | solution.py:375
  4.2 0.0 copy-start.1
  4.2 2.9 %collective-permute-start.1 = (bf16[128,512]{1,0:T(8,128)(2,1)S(1)}, bf16[128,512]{1,0:T(8,128)(2,1)S(1)}, u32[]{:S(2)}, u32[]{:S(2)}) collective-permute-start(bf16[128,512]{1,0:T(8,128)(2,1)S(1)} %get-tuple-element.16), channel_id=1, source_target_pairs={{0,6},{1,7},{2,4},{3,5},{4,2},{5,3},{6,0},{7,1},{8,14},{9,15},{10,... | collective-permute-start | bytes 393224 | tf_op jit(solution)/shard_map/ppermute | solution.py:356
  7.1 0.0 copy-done
  7.1 0.9 %collective-permute-start.6 = (bf16[128,1024]{1,0:T(8,128)(2,1)S(1)}, bf16[128,1024]{1,0:T(8,128)(2,1)S(1)}, u32[]{:S(2)}, u32[]{:S(2)}) collective-permute-start(bf16[128,1024]{1,0:T(8,128)(2,1)S(1)} %copy-done), channel_id=1, source_target_pairs={{0,12},{1,13},{2,14},{3,15},{4,8},{5,9},{6,10},{7,11},{8,4},{9,5},... | collective-permute-start | bytes 786440 | tf_op jit(solution)/shard_map/ppermute | solution.py:356
  8.1 1.8 %collective-permute-start.2 = (bf16[128,1024]{1,0:T(8,128)(2,1)S(1)}, bf16[128,1024]{1,0:T(8,128)(2,1)S(1)}, u32[]{:S(2)}, u32[]{:S(2)}) collective-permute-start(bf16[128,1024]{1,0:T(8,128)(2,1)S(1)} %copy-done), channel_id=1, source_target_pairs={{0,20},{1,21},{2,22},{3,23},{4,16},{5,17},{6,18},{7,19},{8,28},{9,... | collective-permute-start | bytes 786440 | tf_op jit(solution)/shard_map/ppermute | solution.py:356
  9.9 0.0 collective-permute-start.7
  9.9 2.3 %collective-permute-done.5.refs_5_.refs_7_ = bf16[128,1024]{1,0:T(8,128)(2,1)S(1)} collective-permute-done((bf16[128,1024]{1,0:T(8,128)(2,1)}, bf16[128,1024]{1,0:T(8,128)(2,1)S(1)}, u32[]{:S(2)}, u32[]{:S(2)}) %collective-permute-start.5) | collective-permute-done | bytes 262176 | tf_op jit(solution)/shard_map/ppermute | solution.py:356
  12.2 2.8 %collective-permute-start.10 = (bf16[128,1024]{1,0:T(8,128)(2,1)S(1)}, bf16[128,1024]{1,0:T(8,128)(2,1)S(1)}, u32[]{:S(2)}, u32[]{:S(2)}) collective-permute-start(bf16[128,1024]{1,0:T(8,128)(2,1)S(1)} %collective-permute-done.5.refs_5_.refs_7_), channel_id=1, source_target_pairs={{0,12},{1,13},{2,14},{3,15},{4,8},{5,9},{6,10},{7,11},{8,4},{9,5},... | collective-permute-start | bytes 786440 | tf_op jit(solution)/shard_map/ppermute | solution.py:356
  15.0 0.0 collective-permute-done.1.refs_2_
  15.0 1.8 %collective-permute-start = (bf16[128,512]{1,0:T(8,128)(2,1)S(1)}, bf16[128,512]{1,0:T(8,128)(2,1)S(1)}, u32[]{:S(2)}, u32[]{:S(2)}) collective-permute-start(bf16[128,512]{1,0:T(8,128)(2,1)S(1)} %get-tuple-element.17), channel_id=1, source_target_pairs={{0,6},{1,7},{2,4},{3,5},{4,2},{5,3},{6,0},{7,1},{8,14},{9,15},{10,... | collective-permute-start | bytes 393224 | tf_op jit(solution)/shard_map/ppermute | solution.py:356
  16.8 0.0 collective-permute-done.6.refs_6_.refs_8_
  16.8 0.1 collective-permute-start.9
  16.9 7.2 %collective-permute-done.refs_1_ = bf16[128,512]{1,0:T(8,128)(2,1)S(1)} collective-permute-done((bf16[128,512]{1,0:T(8,128)(2,1)S(1)}, bf16[128,512]{1,0:T(8,128)(2,1)S(1)}, u32[]{:S(2)}, u32[]{:S(2)}) %collective-permute-start) | collective-permute-done | bytes 131104 | tf_op jit(solution)/shard_map/ppermute | solution.py:356
  24.1 0.3 collective-permute-start.8
  24.3 0.0 collective-permute-done.2.refs_3_
  24.4 1.4 %collective-permute-start.4 = (bf16[128,512]{1,0:T(8,128)(2,1)S(1)}, bf16[128,512]{1,0:T(8,128)(2,1)S(1)}, u32[]{:S(2)}, u32[]{:S(2)}) collective-permute-start(bf16[128,512]{1,0:T(8,128)(2,1)S(1)} %collective-permute-done.1.refs_2_), channel_id=1, source_target_pairs={{0,20},{1,21},{2,22},{3,23},{4,16},{5,17},{6,18},{7,19},{8,28},{9,... | collective-permute-start | bytes 393224 | tf_op jit(solution)/shard_map/ppermute | solution.py:356
  25.7 0.0 collective-permute-done.7.refs_7_.refs_9_
  25.7 0.4 collective-permute-start.3
  26.1 0.0 collective-permute-done.10.refs_12_
  26.1 0.2 collective-permute-start.11
  26.4 0.0 copy-done.1
  26.4 0.0 collective-permute-done.9.refs_9_.refs_11_
  26.4 0.0 collective-permute-done.8.refs_8_.refs_10_
  26.4 0.1 broadcast_in_dim.13.scales
  26.5 3.6 %shard_map.57 = (f32[3,12,128]{2,1,0:T(8,128)S(1)}, f32[6,2,128,128]{3,2,1,0:T(8,128)S(1)}) custom-call(f32[10,8,128]{2,1,0:T(8,128)S(1)} %broadcast_in_dim.13.scales, s32[8,128]{1,0:T(8,128)S(1)} %broadcast_in_dim.12.place, bf16[128,1024]{1,0:T(8,128)(2,1)S(1)} %copy-done, bf16[128,512]{1,0:T(8,128)(2,1)S(1)} %collective-permute-done.refs_1_, ...), custom_call_target="tpu_custom_call" | custom-call | flops 603979776 | bytes 1179648 | tf_op jit(solution)/shard_map/pallas_call | solution.py:40
  30.1 0.0 collective-permute-done.4.refs_5_
  30.1 2.4 %collective-permute-done.3.refs_4_ = bf16[128,512]{1,0:T(8,128)(2,1)S(1)} collective-permute-done((bf16[128,512]{1,0:T(8,128)(2,1)S(1)}, bf16[128,512]{1,0:T(8,128)(2,1)S(1)}, u32[]{:S(2)}, u32[]{:S(2)}) %collective-permute-start.3) | collective-permute-done | bytes 131104 | tf_op jit(solution)/shard_map/ppermute | solution.py:356
  32.5 0.0 collective-permute-done.11.refs_13_
  32.5 2.3 %shard_map.58 = f32[5,8,128]{2,1,0:T(8,128)S(1)} custom-call(f32[10,8,128]{2,1,0:T(8,128)S(1)} %broadcast_in_dim.13.scales, s32[8,128]{1,0:T(8,128)S(1)} %broadcast_in_dim.12.place, bf16[128,1024]{1,0:T(8,128)(2,1)S(1)} %copy-done, bf16[128,512]{1,0:T(8,128)(2,1)S(1)} %collective-permute-done.refs_1_, bf16[128,512]{1,0:T(8,128)(2,1)S(1)} %collective-permute-done.1.refs_2_, ...), custom_call_target="tpu_custom_call" | custom-call | flops 469762048 | bytes 917504 | tf_op jit(solution)/shard_map/pallas_call | solution.py:40
  34.8 0.1 collective-permute-start.12
  34.9 4.1 %collective-permute-done.12 = f32[5,8,128]{2,1,0:T(8,128)S(1)} collective-permute-done((f32[5,8,128]{2,1,0:T(8,128)S(1)}, f32[5,8,128]{2,1,0:T(8,128)S(1)}, u32[]{:S(2)}, u32[]{:S(2)}) %collective-permute-start.12) | collective-permute-done | bytes 20512 | tf_op jit(solution)/shard_map/ppermute | solution.py:356
  39.0 1.6 %collective-permute-start.13 = (f32[5,8,128]{2,1,0:T(8,128)S(1)}, f32[5,8,128]{2,1,0:T(8,128)S(1)}, u32[]{:S(2)}, u32[]{:S(2)}) collective-permute-start(f32[5,8,128]{2,1,0:T(8,128)S(1)} %add.10), channel_id=1, source_target_pairs={{0,20},{1,21},{2,22},{3,23},{4,16},{5,17},{6,18},{7,19},{8,28},{9,... | collective-permute-start | bytes 61448 | tf_op jit(solution)/shard_map/ppermute | solution.py:356
  40.6 1.6 %collective-permute-done.13 = f32[5,8,128]{2,1,0:T(8,128)S(1)} collective-permute-done((f32[5,8,128]{2,1,0:T(8,128)S(1)}, f32[5,8,128]{2,1,0:T(8,128)S(1)}, u32[]{:S(2)}, u32[]{:S(2)}) %collective-permute-start.13) | collective-permute-done | bytes 20512 | tf_op jit(solution)/shard_map/ppermute | solution.py:356
  42.2 0.5 collective-permute-start.14
  42.7 2.7 %collective-permute-done.14 = f32[1,5,8,128]{3,2,1,0:T(8,128)S(1)} collective-permute-done((f32[1,5,8,128]{3,2,1,0:T(8,128)S(1)}, f32[1,5,8,128]{3,2,1,0:T(8,128)S(1)}, u32[]{:S(2)}, u32[]{:S(2)}) %collective-permute-start.14) | collective-permute-done | bytes 20512 | tf_op jit(solution)/shard_map/ppermute | solution.py:356
  45.4 0.1 collective-permute-start.15
  45.5 3.4 %collective-permute-done.15 = f32[2,5,8,128]{3,2,1,0:T(8,128)S(1)} collective-permute-done((f32[2,5,8,128]{3,2,1,0:T(8,128)S(1)}, f32[2,5,8,128]{3,2,1,0:T(8,128)S(1)}, u32[]{:S(2)}, u32[]{:S(2)}) %collective-permute-start.15) | collective-permute-done | bytes 40992 | tf_op jit(solution)/shard_map/ppermute | solution.py:356
  49.0 0.5 %collective-permute-start.16 = (f32[4,5,8,128]{3,2,1,0:T(8,128)S(1)}, f32[4,5,8,128]{3,2,1,0:T(8,128)S(1)}, u32[]{:S(2)}, u32[]{:S(2)}) collective-permute-start(f32[4,5,8,128]{3,2,1,0:T(8,128)S(1)} %pad_maximum_fusion.1), channel_id=1, source_target_pairs={{0,4},{1,5},{2,6},{3,7},{4,0},{5,1},{6,2},{7,3},{8,12},{9,13},{10,... | collective-permute-start | bytes 245768 | tf_op jit(solution)/shard_map/ppermute | solution.py:356
  49.5 0.9 %collective-permute-done.16 = f32[4,5,8,128]{3,2,1,0:T(8,128)S(1)} collective-permute-done((f32[4,5,8,128]{3,2,1,0:T(8,128)S(1)}, f32[4,5,8,128]{3,2,1,0:T(8,128)S(1)}, u32[]{:S(2)}, u32[]{:S(2)}) %collective-permute-start.16) | collective-permute-done | bytes 81952 | tf_op jit(solution)/shard_map/ppermute | solution.py:356
  50.5 1.2 %shard_map.59 = (f32[10,128]{1,0:T(8,128)}, f32[10,10]{1,0:T(8,128)}, f32[1,10]{1,0:T(1,128)}, f32[1,10]{1,0:T(1,128)}) custom-call(s32[8,128]{1,0:T(8,128)S(1)} %broadcast_in_dim.12.place, f32[8,5,8,128]{3,2,1,0:T(8,128)S(1)} %pad_maximum_fusion.deg, f32[5,8,128]{2,1,0:T(8,128)S(1)} %add.11.own), custom_call_target="tpu_custom_call" | custom-call | tf_op jit(solution)/shard_map/pallas_call | solution.py:40
  (10 shorter events, 0.1 us)
Async XLA Ops:
  0.6 6.5 %copy-start = (bf16[128,1024]{1,0:T(8,128)(2,1)S(1)}, bf16[128,1024]{1,0:T(8,128)(2,1)}, u32[]{:S(2)}) copy-start(bf16[128,1024]{1,0:T(8,128)(2,1)} %refs_6_.1) | copy-start | bytes 786436
  0.6 11.6 %collective-permute-start.5 = (bf16[128,1024]{1,0:T(8,128)(2,1)}, bf16[128,1024]{1,0:T(8,128)(2,1)S(1)}, u32[]{:S(2)}, u32[]{:S(2)}) collective-permute-start(bf16[128,1024]{1,0:T(8,128)(2,1)} %refs_6_.1), channel_id=1, source_target_pairs={{0,5},{1,4},{2,7},{3,6},{4,1},{5,0},{6,3},{7,2},{8,13},{9,12},{10,... | collective-permute-start | bytes 786440 | tf_op jit(solution)/shard_map/ppermute | solution.py:356
  4.2 22.2 %copy-start.1 = (s32[10]{0:T(128)S(1)}, s32[10]{0:T(128)}, u32[]{:S(2)}) copy-start(s32[10]{0:T(128)} %param.3) | copy-start | bytes 124
  4.2 10.8 %collective-permute-start.1 = (bf16[128,512]{1,0:T(8,128)(2,1)S(1)}, bf16[128,512]{1,0:T(8,128)(2,1)S(1)}, u32[]{:S(2)}, u32[]{:S(2)}) collective-permute-start(bf16[128,512]{1,0:T(8,128)(2,1)S(1)} %get-tuple-element.16), channel_id=1, source_target_pairs={{0,6},{1,7},{2,4},{3,5},{4,2},{5,3},{6,0},{7,1},{8,14},{9,15},{10,... | collective-permute-start | bytes 393224 | tf_op jit(solution)/shard_map/ppermute | solution.py:356
  7.1 9.7 %collective-permute-start.6 = (bf16[128,1024]{1,0:T(8,128)(2,1)S(1)}, bf16[128,1024]{1,0:T(8,128)(2,1)S(1)}, u32[]{:S(2)}, u32[]{:S(2)}) collective-permute-start(bf16[128,1024]{1,0:T(8,128)(2,1)S(1)} %copy-done), channel_id=1, source_target_pairs={{0,12},{1,13},{2,14},{3,15},{4,8},{5,9},{6,10},{7,11},{8,4},{9,5},... | collective-permute-start | bytes 786440 | tf_op jit(solution)/shard_map/ppermute | solution.py:356
  8.1 16.3 %collective-permute-start.2 = (bf16[128,1024]{1,0:T(8,128)(2,1)S(1)}, bf16[128,1024]{1,0:T(8,128)(2,1)S(1)}, u32[]{:S(2)}, u32[]{:S(2)}) collective-permute-start(bf16[128,1024]{1,0:T(8,128)(2,1)S(1)} %copy-done), channel_id=1, source_target_pairs={{0,20},{1,21},{2,22},{3,23},{4,16},{5,17},{6,18},{7,19},{8,28},{9,... | collective-permute-start | bytes 786440 | tf_op jit(solution)/shard_map/ppermute | solution.py:356
  9.9 15.8 %collective-permute-start.7 = (bf16[128,1024]{1,0:T(8,128)(2,1)S(1)}, bf16[128,1024]{1,0:T(8,128)(2,1)S(1)}, u32[]{:S(2)}, u32[]{:S(2)}) collective-permute-start(bf16[128,1024]{1,0:T(8,128)(2,1)S(1)} %copy-done), channel_id=1, source_target_pairs={{0,4},{1,5},{2,6},{3,7},{4,0},{5,1},{6,2},{7,3},{8,12},{9,13},{10,... | collective-permute-start | bytes 786440 | tf_op jit(solution)/shard_map/ppermute | solution.py:356
  12.2 13.9 %collective-permute-start.10 = (bf16[128,1024]{1,0:T(8,128)(2,1)S(1)}, bf16[128,1024]{1,0:T(8,128)(2,1)S(1)}, u32[]{:S(2)}, u32[]{:S(2)}) collective-permute-start(bf16[128,1024]{1,0:T(8,128)(2,1)S(1)} %collective-permute-done.5.refs_5_.refs_7_), channel_id=1, source_target_pairs={{0,12},{1,13},{2,14},{3,15},{4,8},{5,9},{6,10},{7,11},{8,4},{9,5},... | collective-permute-start | bytes 786440 | tf_op jit(solution)/shard_map/ppermute | solution.py:356
  15.0 9.1 %collective-permute-start = (bf16[128,512]{1,0:T(8,128)(2,1)S(1)}, bf16[128,512]{1,0:T(8,128)(2,1)S(1)}, u32[]{:S(2)}, u32[]{:S(2)}) collective-permute-start(bf16[128,512]{1,0:T(8,128)(2,1)S(1)} %get-tuple-element.17), channel_id=1, source_target_pairs={{0,6},{1,7},{2,4},{3,5},{4,2},{5,3},{6,0},{7,1},{8,14},{9,15},{10,... | collective-permute-start | bytes 393224 | tf_op jit(solution)/shard_map/ppermute | solution.py:356
  16.8 9.5 %collective-permute-start.9 = (bf16[128,1024]{1,0:T(8,128)(2,1)S(1)}, bf16[128,1024]{1,0:T(8,128)(2,1)S(1)}, u32[]{:S(2)}, u32[]{:S(2)}) collective-permute-start(bf16[128,1024]{1,0:T(8,128)(2,1)S(1)} %collective-permute-done.6.refs_6_.refs_8_), channel_id=1, source_target_pairs={{0,4},{1,5},{2,6},{3,7},{4,0},{5,1},{6,2},{7,3},{8,12},{9,13},{10,... | collective-permute-start | bytes 786440 | tf_op jit(solution)/shard_map/ppermute | solution.py:356
  24.1 2.3 %collective-permute-start.8 = (bf16[128,1024]{1,0:T(8,128)(2,1)S(1)}, bf16[128,1024]{1,0:T(8,128)(2,1)S(1)}, u32[]{:S(2)}, u32[]{:S(2)}) collective-permute-start(bf16[128,1024]{1,0:T(8,128)(2,1)S(1)} %collective-permute-done.5.refs_5_.refs_7_), channel_id=1, source_target_pairs={{0,4},{1,5},{2,6},{3,7},{4,0},{5,1},{6,2},{7,3},{8,12},{9,13},{10,... | collective-permute-start | bytes 786440 | tf_op jit(solution)/shard_map/ppermute | solution.py:356
  24.4 5.8 %collective-permute-start.4 = (bf16[128,512]{1,0:T(8,128)(2,1)S(1)}, bf16[128,512]{1,0:T(8,128)(2,1)S(1)}, u32[]{:S(2)}, u32[]{:S(2)}) collective-permute-start(bf16[128,512]{1,0:T(8,128)(2,1)S(1)} %collective-permute-done.1.refs_2_), channel_id=1, source_target_pairs={{0,20},{1,21},{2,22},{3,23},{4,16},{5,17},{6,18},{7,19},{8,28},{9,... | collective-permute-start | bytes 393224 | tf_op jit(solution)/shard_map/ppermute | solution.py:356
  25.7 6.8 %collective-permute-start.3 = (bf16[128,512]{1,0:T(8,128)(2,1)S(1)}, bf16[128,512]{1,0:T(8,128)(2,1)S(1)}, u32[]{:S(2)}, u32[]{:S(2)}) collective-permute-start(bf16[128,512]{1,0:T(8,128)(2,1)S(1)} %collective-permute-done.refs_1_), channel_id=1, source_target_pairs={{0,20},{1,21},{2,22},{3,23},{4,16},{5,17},{6,18},{7,19},{8,28},{9,... | collective-permute-start | bytes 393224 | tf_op jit(solution)/shard_map/ppermute | solution.py:356
  26.1 6.4 %collective-permute-start.11 = (bf16[128,1024]{1,0:T(8,128)(2,1)S(1)}, bf16[128,1024]{1,0:T(8,128)(2,1)S(1)}, u32[]{:S(2)}, u32[]{:S(2)}) collective-permute-start(bf16[128,1024]{1,0:T(8,128)(2,1)S(1)} %collective-permute-done.10.refs_12_), channel_id=1, source_target_pairs={{0,4},{1,5},{2,6},{3,7},{4,0},{5,1},{6,2},{7,3},{8,12},{9,13},{10,... | collective-permute-start | bytes 786440 | tf_op jit(solution)/shard_map/ppermute | solution.py:356
  34.8 4.2 %collective-permute-start.12 = (f32[5,8,128]{2,1,0:T(8,128)S(1)}, f32[5,8,128]{2,1,0:T(8,128)S(1)}, u32[]{:S(2)}, u32[]{:S(2)}) collective-permute-start(f32[5,8,128]{2,1,0:T(8,128)S(1)} %shard_map.58), channel_id=1, source_target_pairs={{0,6},{1,7},{2,4},{3,5},{4,2},{5,3},{6,0},{7,1},{8,14},{9,15},{10,... | collective-permute-start | bytes 61448 | tf_op jit(solution)/shard_map/ppermute | solution.py:356
  39.0 3.2 %collective-permute-start.13 = (f32[5,8,128]{2,1,0:T(8,128)S(1)}, f32[5,8,128]{2,1,0:T(8,128)S(1)}, u32[]{:S(2)}, u32[]{:S(2)}) collective-permute-start(f32[5,8,128]{2,1,0:T(8,128)S(1)} %add.10), channel_id=1, source_target_pairs={{0,20},{1,21},{2,22},{3,23},{4,16},{5,17},{6,18},{7,19},{8,28},{9,... | collective-permute-start | bytes 61448 | tf_op jit(solution)/shard_map/ppermute | solution.py:356
  42.2 3.2 %collective-permute-start.14 = (f32[1,5,8,128]{3,2,1,0:T(8,128)S(1)}, f32[1,5,8,128]{3,2,1,0:T(8,128)S(1)}, u32[]{:S(2)}, u32[]{:S(2)}) collective-permute-start(f32[1,5,8,128]{3,2,1,0:T(8,128)S(1)} %bitcast.5), channel_id=1, source_target_pairs={{0,5},{1,4},{2,7},{3,6},{4,1},{5,0},{6,3},{7,2},{8,13},{9,12},{10,... | collective-permute-start | bytes 61448 | tf_op jit(solution)/shard_map/ppermute | solution.py:356
  45.4 3.5 %collective-permute-start.15 = (f32[2,5,8,128]{3,2,1,0:T(8,128)S(1)}, f32[2,5,8,128]{3,2,1,0:T(8,128)S(1)}, u32[]{:S(2)}, u32[]{:S(2)}) collective-permute-start(f32[2,5,8,128]{3,2,1,0:T(8,128)S(1)} %pad_maximum_fusion.2), channel_id=1, source_target_pairs={{0,12},{1,13},{2,14},{3,15},{4,8},{5,9},{6,10},{7,11},{8,4},{9,5},... | collective-permute-start | bytes 122888 | tf_op jit(solution)/shard_map/ppermute | solution.py:356
  49.0 1.5 %collective-permute-start.16 = (f32[4,5,8,128]{3,2,1,0:T(8,128)S(1)}, f32[4,5,8,128]{3,2,1,0:T(8,128)S(1)}, u32[]{:S(2)}, u32[]{:S(2)}) collective-permute-start(f32[4,5,8,128]{3,2,1,0:T(8,128)S(1)} %pad_maximum_fusion.1), channel_id=1, source_target_pairs={{0,4},{1,5},{2,6},{3,7},{4,0},{5,1},{6,2},{7,3},{8,12},{9,13},{10,... | collective-permute-start | bytes 245768 | tf_op jit(solution)/shard_map/ppermute | solution.py:356

commit v3 on v2

--- a/solution.py
+++ b/solution.py
@@ -36,11 +36,12 @@
     return pl.BlockSpec(memory_space=pltpu.VMEM)
 
 
-def pallas(kernel, out_shape, operands, scratch=(), cost=None):
+def pallas(kernel, out_shape, operands, scratch=(), cost=None, scalars=0):
     return pl.pallas_call(
         kernel,
         out_shape=out_shape,
-        in_specs=[vmem_spec()] * len(operands),
+        in_specs=[pl.BlockSpec(memory_space=pltpu.SMEM)] * scalars
+        + [vmem_spec()] * (len(operands) - scalars),
         out_specs=jax.tree.map(lambda _: vmem_spec(), out_shape),
         scratch_shapes=list(scratch),
         compiler_params=pltpu.CompilerParams(vmem_limit_bytes=VMEM_LIMIT),
@@ -96,34 +97,63 @@
         )
 
 
-def early_kernel(lane_sizes, sub_count, scales, place, *refs):
-    lanes, refs = split_refs(refs, lane_sizes)
-    subs, (out, sub_stats, raw) = refs[:sub_count], refs[sub_count:]
-    _, _, genes = scales.shape
-    blocks = [whole(parts) for parts in lanes]
-    multiply(raw, subs, jnp.concatenate(blocks, axis=0))
+def first_kernel(sub_count, powers, lane, *refs):
+    subs, (scales, out, sub_stats, raw) = refs[:sub_count], refs[sub_count:]
+    npower, tile, genes = scales.shape
+    for p in range(npower):
+        scales[p] = jnp.full((tile, genes), powers[p].astype(jnp.float32) * LOG2E)
+    block = lane[...]
+    multiply(raw, subs, block)
     for b, sub in enumerate(subs):
         measure_sub(sub[...], sub_stats.at[b])
+    mean, inv = gene_stats(block)
+    mean, inv = as_row(mean), as_row(inv)
     stat_refs = [sub_stats.at[b] for b in range(sub_count)]
+    rows = row_sums(raw, slice(0, genes), stat_refs, mean, inv, scales)
+    for p, row in enumerate(rows + [mean, inv]):
+        out[0, p : p + 1, :] = row
+
+
+def early_kernel(lane_sizes, known_count, new_count, scales, place, *refs):
+    lanes, refs = split_refs(refs, lane_sizes)
+    (known, new), refs = split_refs(refs, (known_count, new_count))
+    stat_refs = []
+    if known_count:
+        stat_refs, refs = [refs[0].at[b] for b in range(known_count)], refs[1:]
+    prior, out, new_stats, raw = refs
+    npower, _, genes = scales.shape
+    blocks = [whole(parts) for parts in lanes]
+    multiply(raw, new + known, jnp.concatenate(blocks, axis=0))
+    for b, sub in enumerate(new):
+        measure_sub(sub[...], new_stats.at[b])
+    new_refs = [new_stats.at[b] for b in range(new_count)]
     for a, block in enumerate(blocks):
-        mean, inv = gene_stats(block)
-        mean, inv = as_row(mean), as_row(inv)
         column = slice(a * genes, (a + 1) * genes)
-        rows = row_sums(raw, column, stat_refs, mean, inv, scales)
+        if a < prior.shape[0]:
+            begun = [prior[a, p : p + 1, :] for p in range(npower + 2)]
+            mean, inv = begun[npower:]
+            rows = row_sums(raw, column, new_refs, mean, inv, scales)
+            rows = [row + begun[p] for p, row in enumerate(rows)]
+        else:
+            mean, inv = gene_stats(block)
+            mean, inv = as_row(mean), as_row(inv)
+            rows = row_sums(raw, column, new_refs + stat_refs, mean, inv, scales)
         for p, row in enumerate(rows + [mean, inv]):
             out[a, p : p + 1, :] = row
 
 
-def late_kernel(here_sizes, last_sizes, first_count, second_count, scales, place, *refs):
+def late_kernel(here_sizes, last_sizes, counts, second_count, scales, place, *refs):
     here, refs = split_refs(refs, here_sizes)
     last, refs = split_refs(refs, last_sizes)
-    (first, second), refs = split_refs(refs, (first_count, second_count))
-    first_stats, prior, out, raw_here, raw_last, second_stats = refs
+    (first, second), refs = split_refs(refs, (sum(counts), second_count))
+    stat_arrays, refs = refs[: len(counts)], refs[len(counts) :]
+    prior, out, raw_here, raw_last, second_stats = refs
     npower, _, genes = scales.shape
     slots = len(here) + len(last)
     full, rest = npower // TILE, npower % TILE
     second_refs = [second_stats.at[b] for b in range(second_count)]
-    all_refs = [first_stats.at[b] for b in range(first_count)] + second_refs
+    all_refs = [ref.at[b] for ref, count in zip(stat_arrays, counts) for b in range(count)]
+    all_refs += second_refs
     rows = []
     multiply(raw_here, second, jnp.concatenate([whole(parts) for parts in here], axis=0))
     for b, sub in enumerate(second):
@@ -176,15 +206,33 @@
     return [len(parts) for parts in blocks]
 
 
-def early_sums(scales, place, here, first):
-    genes, samples = first[0].shape
+def first_sums(powers, lane, subs):
+    genes, samples = lane.shape
+    npower = powers.shape[0]
+    return pallas(
+        functools.partial(first_kernel, len(subs)),
+        (
+            f32(npower, TILE, genes),
+            f32(1, npower + 2, genes),
+            f32(len(subs), 2, genes, genes),
+        ),
+        [powers, lane] + subs,
+        [pltpu.VMEM((len(subs), genes, genes), jnp.float32)],
+        work(len(subs) * genes * genes, samples, npower),
+        scalars=1,
+    )
+
+
+def early_sums(scales, place, here, known, new, known_stats, prior):
+    genes, samples = new[0].shape
     npower = scales.shape[0]
+    count = len(known) + len(new)
     return pallas(
-        functools.partial(early_kernel, sizes_of(here), len(first)),
-        (f32(len(here), npower + 2, genes), f32(len(first), 2, genes, genes)),
-        [scales, place] + flat(here) + first,
-        [pltpu.VMEM((len(first), genes, len(here) * genes), jnp.float32)],
-        work(len(here) * len(first) * genes * genes, samples, npower),
+        functools.partial(early_kernel, sizes_of(here), len(known), len(new)),
+        (f32(len(here), npower + 2, genes), f32(len(new), 2, genes, genes)),
+        [scales, place] + flat(here) + known + new + known_stats + [prior],
+        [pltpu.VMEM((count, genes, len(here) * genes), jnp.float32)],
+        work(len(here) * count * genes * genes, samples, npower),
     )
 
 
@@ -194,10 +242,14 @@
     blocks = len(here) * len(second) + len(last) * (len(first) + len(second))
     return pallas(
         functools.partial(
-            late_kernel, sizes_of(here), sizes_of(last), len(first), len(second)
+            late_kernel,
+            sizes_of(here),
+            sizes_of(last),
+            [array.shape[0] for array in first_stats],
+            len(second),
         ),
         f32(tile_count(npower, len(here) + len(last)), TILE, genes),
-        [scales, place] + flat(here) + flat(last) + first + second + [first_stats, prior],
+        [scales, place] + flat(here) + flat(last) + first + second + first_stats + [prior],
         [
             pltpu.VMEM((len(second), genes, len(here) * genes), jnp.float32),
             pltpu.VMEM((len(first) + len(second), genes, len(last) * genes), jnp.float32),
@@ -367,9 +419,6 @@
     upper.append(parity)
     genes, samples = expression.shape
     place = jnp.broadcast_to(mine, (TILE, genes))
-    scales = jnp.broadcast_to(
-        (powers.astype(jnp.float32) * LOG2E)[:, None, None], (npower, TILE, genes)
-    )
 
     width = samples // PIECES
     pieces = tuple(expression[:, i * width : (i + 1) * width] for i in range(PIECES))
@@ -388,10 +437,17 @@
     quarter = max(len(lane_blocks) // 4, 1)
     here, last = lane_blocks[:-quarter], lane_blocks[-quarter:]
     quarter = max(len(sub_blocks) // 4, 1)
-    first = sub_blocks[:-quarter] + crossed[:-quarter]
-    second = sub_blocks[-quarter:] + crossed[-quarter:]
-    part, first_stats = early_sums(scales, place, here, first)
-    part = late_sums(scales, place, here, last, first, second, first_stats, part)
+    known = [sub_blocks[0], crossed[0]]
+    new = sub_blocks[1:-quarter] + crossed[1:-quarter]
+    second, third = sub_blocks[-quarter:], crossed[-quarter:]
+    scales, part, stats = first_sums(powers, expression, known)
+    stats = [stats]
+    part, new_stats = early_sums(scales, place, here, known, new, stats, part)
+    stats.append(new_stats)
+    part, new_stats = early_sums(scales, place, here, [], second, [], part)
+    stats.append(new_stats)
+    ready = known + new + second
+    part = late_sums(scales, place, here, last, ready, third, stats, part)
 
     for bit in far:
         part = part + from_partner(part, bit)

time: 51.8 us -> 51.9 us (level)
  waiting for transfers between devices: 24.7 us -> 20.6 us
  starting transfers between devices: 17.9 us -> 20.8 us
  Pallas kernels: 7.1 us -> 7.8 us
  local copies, waits for them, and re-layouts: 1.08 us -> 1.66 us
    ppermute x17, waiting for transfers between devices: 24.7 us -> 20.6 us  [from_partner(): return lax.ppermute(array, AXES, [(i, i ^ bit) for i in range(devices)])]
    ppermute x17, starting transfers between devices: 17.9 us -> 20.8 us  [from_partner(): return lax.ppermute(array, AXES, [(i, i ^ bit) for i in range(devices)])]
    pallas_call x3 -> x5, Pallas kernels: 7.1 us -> 7.8 us  [pallas(): pl.pallas_call(kernel, out_shape=out_shape, in_specs=[pl.BlockSpec(memory...]
    unnamed x4, local copies, waits for them, and re-layouts: 0.01 us -> 0.66 us
  transfers between devices with their start and end apart: 17 -> 17, of which waited for: 8 -> 8; matrix products, arithmetic and copies ran while one was open for 2% -> 2% of each run, Pallas kernels for 7% -> 9%
where the time goes in v3:
time: 51.9 us; the launch traced here: 51.7 us
  starting transfers between devices  20.8 us (40%)
  waiting for transfers between devices  20.6 us (40%)
  Pallas kernels  7.8 us (15%)
  local copies, waits for them, and re-layouts  1.66 us (3%)
  between operations  0.75 us (1%)
    ppermute x17, starting transfers between devices, from_partner(): return lax.ppermute(array, AXES, [(i, i ^ bit) for i in range(devices)])  20.8 us
    ppermute x17, waiting for transfers between devices, from_partner(): return lax.ppermute(array, AXES, [(i, i ^ bit) for i in range(devices)])  20.6 us
    pallas_call x5, Pallas kernels, pallas(): pl.pallas_call(kernel, out_shape=out_shape, in_specs=[pl.BlockSpec(memory...  7.8 us
  transfers between devices with their start and end apart: 17, of which 8 were waited for; matrix products, arithmetic and copies ran while one was open for 2% of the time, Pallas kernels for 9%

profile of v3, /device:TPU:0, one launch (start us, length us, event | category | flops | bytes accessed | tf_op | source)
XLA Modules:
  0.0 51.7 jit_solution(2706675818606405574)
XLA Ops:
  0.6 0.0 copy-start
  0.6 2.6 %collective-permute-start.6 = (bf16[128,1024]{1,0:T(8,128)(2,1)}, bf16[128,1024]{1,0:T(8,128)(2,1)S(1)}, u32[]{:S(2)}, u32[]{:S(2)}) collective-permute-start(bf16[128,1024]{1,0:T(8,128)(2,1)} %refs_6_.1), channel_id=1, source_target_pairs={{0,5},{1,4},{2,7},{3,6},{4,1},{5,0},{6,3},{7,2},{8,13},{9,12},{10,... | collective-permute-start | bytes 786440 | tf_op jit(solution)/shard_map/ppermute | solution.py:408
  3.2 1.8 %collective-permute-start.7 = (bf16[128,1024]{1,0:T(8,128)(2,1)}, bf16[128,1024]{1,0:T(8,128)(2,1)S(1)}, u32[]{:S(2)}, u32[]{:S(2)}) collective-permute-start(bf16[128,1024]{1,0:T(8,128)(2,1)} %refs_6_.1), channel_id=1, source_target_pairs={{0,12},{1,13},{2,14},{3,15},{4,8},{5,9},{6,10},{7,11},{8,4},{9,5},... | collective-permute-start | bytes 786440 | tf_op jit(solution)/shard_map/ppermute | solution.py:408
  5.0 1.0 %fusion = (bf16[128,512]{1,0:T(8,128)(2,1)S(1)}, bf16[128,512]{1,0:T(8,128)(2,1)S(1)}) fusion(bf16[128,1024]{1,0:T(8,128)(2,1)} %refs_6_.1), kind=kLoop, calls=%fused_computation.9 | loop fusion | bytes 524288 | tf_op jit(solution)/shard_map/slice | solution.py:424
  6.0 2.1 %collective-permute-start.1 = (bf16[128,512]{1,0:T(8,128)(2,1)S(1)}, bf16[128,512]{1,0:T(8,128)(2,1)S(1)}, u32[]{:S(2)}, u32[]{:S(2)}) collective-permute-start(bf16[128,512]{1,0:T(8,128)(2,1)S(1)} %get-tuple-element.27), channel_id=1, source_target_pairs={{0,6},{1,7},{2,4},{3,5},{4,2},{5,3},{6,0},{7,1},{8,14},{9,15},{10,... | collective-permute-start | bytes 393224 | tf_op jit(solution)/shard_map/ppermute | solution.py:408
  8.1 2.1 %collective-permute-done.6.refs_6_.refs_8_ = bf16[128,1024]{1,0:T(8,128)(2,1)S(1)} collective-permute-done((bf16[128,1024]{1,0:T(8,128)(2,1)}, bf16[128,1024]{1,0:T(8,128)(2,1)S(1)}, u32[]{:S(2)}, u32[]{:S(2)}) %collective-permute-start.6) | collective-permute-done | bytes 262176 | tf_op jit(solution)/shard_map/ppermute | solution.py:408
  10.2 4.7 %collective-permute-start.10 = (bf16[128,1024]{1,0:T(8,128)(2,1)S(1)}, bf16[128,1024]{1,0:T(8,128)(2,1)S(1)}, u32[]{:S(2)}, u32[]{:S(2)}) collective-permute-start(bf16[128,1024]{1,0:T(8,128)(2,1)S(1)} %collective-permute-done.6.refs_6_.refs_8_), channel_id=1, source_target_pairs={{0,12},{1,13},{2,14},{3,15},{4,8},{5,9},{6,10},{7,11},{8,4},{9,5},... | collective-permute-start | bytes 786440 | tf_op jit(solution)/shard_map/ppermute | solution.py:408
  14.9 1.9 %collective-permute-start.2 = (bf16[128,512]{1,0:T(8,128)(2,1)S(1)}, bf16[128,512]{1,0:T(8,128)(2,1)S(1)}, u32[]{:S(2)}, u32[]{:S(2)}) collective-permute-start(bf16[128,512]{1,0:T(8,128)(2,1)S(1)} %get-tuple-element.26), channel_id=1, source_target_pairs={{0,6},{1,7},{2,4},{3,5},{4,2},{5,3},{6,0},{7,1},{8,14},{9,15},{10,... | collective-permute-start | bytes 393224 | tf_op jit(solution)/shard_map/ppermute | solution.py:408
  16.8 0.0 copy-done
  16.8 0.1 collective-permute-start
  16.9 0.0 collective-permute-done.1.refs_1_
  16.9 1.5 %collective-permute-start.3 = (bf16[128,1024]{1,0:T(8,128)(2,1)S(1)}, bf16[128,1024]{1,0:T(8,128)(2,1)S(1)}, u32[]{:S(2)}, u32[]{:S(2)}) collective-permute-start(bf16[128,1024]{1,0:T(8,128)(2,1)S(1)} %copy-done), channel_id=1, source_target_pairs={{0,20},{1,21},{2,22},{3,23},{4,16},{5,17},{6,18},{7,19},{8,28},{9,... | collective-permute-start | bytes 786440 | tf_op jit(solution)/shard_map/ppermute | solution.py:408
  18.4 5.4 %collective-permute-done.2.refs_2_ = bf16[128,512]{1,0:T(8,128)(2,1)S(1)} collective-permute-done((bf16[128,512]{1,0:T(8,128)(2,1)S(1)}, bf16[128,512]{1,0:T(8,128)(2,1)S(1)}, u32[]{:S(2)}, u32[]{:S(2)}) %collective-permute-start.2) | collective-permute-done | bytes 131104 | tf_op jit(solution)/shard_map/ppermute | solution.py:408
  23.8 0.4 collective-permute-start.8
  24.2 0.0 collective-permute-done.7.refs_7_.refs_9_
  24.2 0.1 collective-permute-start.9
  24.3 0.0 collective-permute-done.10.refs_4_.refs_12_
  24.3 0.4 collective-permute-start.11
  24.7 0.0 collective-permute-done.refs_1_.refs_5_.refs_7_
  24.7 1.2 %collective-permute-start.4 = (bf16[128,512]{1,0:T(8,128)(2,1)S(1)}, bf16[128,512]{1,0:T(8,128)(2,1)S(1)}, u32[]{:S(2)}, u32[]{:S(2)}) collective-permute-start(bf16[128,512]{1,0:T(8,128)(2,1)S(1)} %collective-permute-done.1.refs_1_), channel_id=1, source_target_pairs={{0,20},{1,21},{2,22},{3,23},{4,16},{5,17},{6,18},{7,19},{8,28},{9,... | collective-permute-start | bytes 393224 | tf_op jit(solution)/shard_map/ppermute | solution.py:408
  26.0 0.0 collective-permute-done.3.refs_3_
  26.0 0.5 collective-permute-start.5
  26.5 0.0 copy-start.1
  26.5 0.7 %copy-done.1 = s32[10]{0:T(128)S(1)} copy-done((s32[10]{0:T(128)S(1)}, s32[10]{0:T(128)}, u32[]{:S(2)}) %copy-start.1) | copy-done | bytes 64
  27.1 1.2 %shard_map.57 = (f32[10,8,128]{2,1,0:T(8,128)S(1)}, f32[1,12,128]{2,1,0:T(8,128)S(1)}, f32[2,2,128,128]{3,2,1,0:T(8,128)S(1)}) custom-call(s32[10]{0:T(128)S(1)} %copy-done.1, bf16[128,1024]{1,0:T(8,128)(2,1)S(1)} %copy-done, bf16[128,1024]{1,0:T(8,128)(2,1)S(1)} %copy-done, bf16[128,1024]{1,0:T(8,128)(2,1)S(1)} %collective-permute-done.refs_1_.refs_5_.refs_7_), custom_call_target="tpu_custom_call" | custom-call | flops 67108864 | bytes 131072 | tf_op jit(solution)/shard_map/pallas_call | solution.py:40
  28.4 0.0 collective-permute-done.8.refs_8_.refs_10_
  28.4 0.0 collective-permute-done.9.refs_9_.refs_11_
  28.4 2.9 %shard_map.58 = (f32[3,12,128]{2,1,0:T(8,128)S(1)}, f32[4,2,128,128]{3,2,1,0:T(8,128)S(1)}) custom-call(f32[10,8,128]{2,1,0:T(8,128)S(1)} %get-tuple-element.15.scales, s32[8,128]{1,0:T(8,128)S(1)} %broadcast_in_dim.6.place, bf16[128,1024]{1,0:T(8,128)(2,1)S(1)} %copy-done, bf16[128,512]{1,0:T(8,128)(2,1)S(1)} %collective-permute-done.1.refs_1_, ...), custom_call_target="tpu_custom_call" | custom-call | flops 603979776 | bytes 1179648 | tf_op jit(solution)/shard_map/pallas_call | solution.py:40
  31.3 0.7 %shard_map.59 = (f32[3,12,128]{2,1,0:T(8,128)S(1)}, f32[1,2,128,128]{3,2,1,0:T(8,128)S(1)}) custom-call(f32[10,8,128]{2,1,0:T(8,128)S(1)} %get-tuple-element.15.scales, s32[8,128]{1,0:T(8,128)S(1)} %broadcast_in_dim.6.place, bf16[128,1024]{1,0:T(8,128)(2,1)S(1)} %copy-done, bf16[128,512]{1,0:T(8,128)(2,1)S(1)} %collective-permute-done.1.refs_1_, ...), custom_call_target="tpu_custom_call" | custom-call | flops 100663296 | bytes 196608 | tf_op jit(solution)/shard_map/pallas_call | solution.py:40
  32.0 0.0 collective-permute-done.4.refs_4_
  32.0 1.0 %collective-permute-done.5.refs_5_ = bf16[128,512]{1,0:T(8,128)(2,1)S(1)} collective-permute-done((bf16[128,512]{1,0:T(8,128)(2,1)S(1)}, bf16[128,512]{1,0:T(8,128)(2,1)S(1)}, u32[]{:S(2)}, u32[]{:S(2)}) %collective-permute-start.5) | collective-permute-done | bytes 131104 | tf_op jit(solution)/shard_map/ppermute | solution.py:408
  33.0 0.0 collective-permute-done.11.refs_13_
  33.0 1.8 %shard_map.60 = f32[5,8,128]{2,1,0:T(8,128)S(1)} custom-call(f32[10,8,128]{2,1,0:T(8,128)S(1)} %get-tuple-element.15.scales, s32[8,128]{1,0:T(8,128)S(1)} %broadcast_in_dim.6.place, bf16[128,1024]{1,0:T(8,128)(2,1)S(1)} %copy-done, bf16[128,512]{1,0:T(8,128)(2,1)S(1)} %collective-permute-done.1.refs_1_, bf16[128,512]{1,0:T(8,128)(2,1)S(1)} %collective-permute-done.2.refs_2_, ...), custom_call_target="tpu_custom_call" | custom-call | flops 369098752 | bytes 720896 | tf_op jit(solution)/shard_map/pallas_call | solution.py:40
  34.9 0.1 collective-permute-start.12
  34.9 4.1 %collective-permute-done.12 = f32[5,8,128]{2,1,0:T(8,128)S(1)} collective-permute-done((f32[5,8,128]{2,1,0:T(8,128)S(1)}, f32[5,8,128]{2,1,0:T(8,128)S(1)}, u32[]{:S(2)}, u32[]{:S(2)}) %collective-permute-start.12) | collective-permute-done | bytes 20512 | tf_op jit(solution)/shard_map/ppermute | solution.py:408
  39.0 1.6 %collective-permute-start.13 = (f32[5,8,128]{2,1,0:T(8,128)S(1)}, f32[5,8,128]{2,1,0:T(8,128)S(1)}, u32[]{:S(2)}, u32[]{:S(2)}) collective-permute-start(f32[5,8,128]{2,1,0:T(8,128)S(1)} %add.10), channel_id=1, source_target_pairs={{0,20},{1,21},{2,22},{3,23},{4,16},{5,17},{6,18},{7,19},{8,28},{9,... | collective-permute-start | bytes 61448 | tf_op jit(solution)/shard_map/ppermute | solution.py:408
  40.6 1.6 %collective-permute-done.13 = f32[5,8,128]{2,1,0:T(8,128)S(1)} collective-permute-done((f32[5,8,128]{2,1,0:T(8,128)S(1)}, f32[5,8,128]{2,1,0:T(8,128)S(1)}, u32[]{:S(2)}, u32[]{:S(2)}) %collective-permute-start.13) | collective-permute-done | bytes 20512 | tf_op jit(solution)/shard_map/ppermute | solution.py:408
  42.2 1.1 %collective-permute-start.14 = (f32[1,5,8,128]{3,2,1,0:T(8,128)S(1)}, f32[1,5,8,128]{3,2,1,0:T(8,128)S(1)}, u32[]{:S(2)}, u32[]{:S(2)}) collective-permute-start(f32[1,5,8,128]{3,2,1,0:T(8,128)S(1)} %bitcast.5), channel_id=1, source_target_pairs={{0,5},{1,4},{2,7},{3,6},{4,1},{5,0},{6,3},{7,2},{8,13},{9,12},{10,... | collective-permute-start | bytes 61448 | tf_op jit(solution)/shard_map/ppermute | solution.py:408
  43.3 2.1 %collective-permute-done.14 = f32[1,5,8,128]{3,2,1,0:T(8,128)S(1)} collective-permute-done((f32[1,5,8,128]{3,2,1,0:T(8,128)S(1)}, f32[1,5,8,128]{3,2,1,0:T(8,128)S(1)}, u32[]{:S(2)}, u32[]{:S(2)}) %collective-permute-start.14) | collective-permute-done | bytes 20512 | tf_op jit(solution)/shard_map/ppermute | solution.py:408
  45.5 0.6 %collective-permute-start.15 = (f32[2,5,8,128]{3,2,1,0:T(8,128)S(1)}, f32[2,5,8,128]{3,2,1,0:T(8,128)S(1)}, u32[]{:S(2)}, u32[]{:S(2)}) collective-permute-start(f32[2,5,8,128]{3,2,1,0:T(8,128)S(1)} %pad_maximum_fusion.2), channel_id=1, source_target_pairs={{0,12},{1,13},{2,14},{3,15},{4,8},{5,9},{6,10},{7,11},{8,4},{9,5},... | collective-permute-start | bytes 122888 | tf_op jit(solution)/shard_map/ppermute | solution.py:408
  46.1 3.0 %collective-permute-done.15 = f32[2,5,8,128]{3,2,1,0:T(8,128)S(1)} collective-permute-done((f32[2,5,8,128]{3,2,1,0:T(8,128)S(1)}, f32[2,5,8,128]{3,2,1,0:T(8,128)S(1)}, u32[]{:S(2)}, u32[]{:S(2)}) %collective-permute-start.15) | collective-permute-done | bytes 40992 | tf_op jit(solution)/shard_map/ppermute | solution.py:408
  49.1 0.2 collective-permute-start.16
  49.3 1.2 %collective-permute-done.16 = f32[4,5,8,128]{3,2,1,0:T(8,128)S(1)} collective-permute-done((f32[4,5,8,128]{3,2,1,0:T(8,128)S(1)}, f32[4,5,8,128]{3,2,1,0:T(8,128)S(1)}, u32[]{:S(2)}, u32[]{:S(2)}) %collective-permute-start.16) | collective-permute-done | bytes 81952 | tf_op jit(solution)/shard_map/ppermute | solution.py:408
  50.5 1.2 %shard_map.61 = (f32[10,128]{1,0:T(8,128)}, f32[10,10]{1,0:T(8,128)}, f32[1,10]{1,0:T(1,128)}, f32[1,10]{1,0:T(1,128)}) custom-call(s32[8,128]{1,0:T(8,128)S(1)} %broadcast_in_dim.6.place, f32[8,5,8,128]{3,2,1,0:T(8,128)S(1)} %pad_maximum_fusion.deg, f32[5,8,128]{2,1,0:T(8,128)S(1)} %add.11.own), custom_call_target="tpu_custom_call" | custom-call | tf_op jit(solution)/shard_map/pallas_call | solution.py:40
  (9 shorter events, 0.1 us)
Async XLA Ops:
  0.6 16.2 %copy-start = (bf16[128,1024]{1,0:T(8,128)(2,1)S(1)}, bf16[128,1024]{1,0:T(8,128)(2,1)}, u32[]{:S(2)}) copy-start(bf16[128,1024]{1,0:T(8,128)(2,1)} %refs_6_.1) | copy-start | bytes 786436
  0.6 9.6 %collective-permute-start.6 = (bf16[128,1024]{1,0:T(8,128)(2,1)}, bf16[128,1024]{1,0:T(8,128)(2,1)S(1)}, u32[]{:S(2)}, u32[]{:S(2)}) collective-permute-start(bf16[128,1024]{1,0:T(8,128)(2,1)} %refs_6_.1), channel_id=1, source_target_pairs={{0,5},{1,4},{2,7},{3,6},{4,1},{5,0},{6,3},{7,2},{8,13},{9,12},{10,... | collective-permute-start | bytes 786440 | tf_op jit(solution)/shard_map/ppermute | solution.py:408
  3.2 21.0 %collective-permute-start.7 = (bf16[128,1024]{1,0:T(8,128)(2,1)}, bf16[128,1024]{1,0:T(8,128)(2,1)S(1)}, u32[]{:S(2)}, u32[]{:S(2)}) collective-permute-start(bf16[128,1024]{1,0:T(8,128)(2,1)} %refs_6_.1), channel_id=1, source_target_pairs={{0,12},{1,13},{2,14},{3,15},{4,8},{5,9},{6,10},{7,11},{8,4},{9,5},... | collective-permute-start | bytes 786440 | tf_op jit(solution)/shard_map/ppermute | solution.py:408
  6.0 10.9 %collective-permute-start.1 = (bf16[128,512]{1,0:T(8,128)(2,1)S(1)}, bf16[128,512]{1,0:T(8,128)(2,1)S(1)}, u32[]{:S(2)}, u32[]{:S(2)}) collective-permute-start(bf16[128,512]{1,0:T(8,128)(2,1)S(1)} %get-tuple-element.27), channel_id=1, source_target_pairs={{0,6},{1,7},{2,4},{3,5},{4,2},{5,3},{6,0},{7,1},{8,14},{9,15},{10,... | collective-permute-start | bytes 393224 | tf_op jit(solution)/shard_map/ppermute | solution.py:408
  10.2 14.1 %collective-permute-start.10 = (bf16[128,1024]{1,0:T(8,128)(2,1)S(1)}, bf16[128,1024]{1,0:T(8,128)(2,1)S(1)}, u32[]{:S(2)}, u32[]{:S(2)}) collective-permute-start(bf16[128,1024]{1,0:T(8,128)(2,1)S(1)} %collective-permute-done.6.refs_6_.refs_8_), channel_id=1, source_target_pairs={{0,12},{1,13},{2,14},{3,15},{4,8},{5,9},{6,10},{7,11},{8,4},{9,5},... | collective-permute-start | bytes 786440 | tf_op jit(solution)/shard_map/ppermute | solution.py:408
  14.9 8.9 %collective-permute-start.2 = (bf16[128,512]{1,0:T(8,128)(2,1)S(1)}, bf16[128,512]{1,0:T(8,128)(2,1)S(1)}, u32[]{:S(2)}, u32[]{:S(2)}) collective-permute-start(bf16[128,512]{1,0:T(8,128)(2,1)S(1)} %get-tuple-element.26), channel_id=1, source_target_pairs={{0,6},{1,7},{2,4},{3,5},{4,2},{5,3},{6,0},{7,1},{8,14},{9,15},{10,... | collective-permute-start | bytes 393224 | tf_op jit(solution)/shard_map/ppermute | solution.py:408
  16.8 7.9 %collective-permute-start = (bf16[128,1024]{1,0:T(8,128)(2,1)S(1)}, bf16[128,1024]{1,0:T(8,128)(2,1)S(1)}, u32[]{:S(2)}, u32[]{:S(2)}) collective-permute-start(bf16[128,1024]{1,0:T(8,128)(2,1)S(1)} %copy-done), channel_id=1, source_target_pairs={{0,4},{1,5},{2,6},{3,7},{4,0},{5,1},{6,2},{7,3},{8,12},{9,13},{10,... | collective-permute-start | bytes 786440 | tf_op jit(solution)/shard_map/ppermute | solution.py:408
  16.9 9.1 %collective-permute-start.3 = (bf16[128,1024]{1,0:T(8,128)(2,1)S(1)}, bf16[128,1024]{1,0:T(8,128)(2,1)S(1)}, u32[]{:S(2)}, u32[]{:S(2)}) collective-permute-start(bf16[128,1024]{1,0:T(8,128)(2,1)S(1)} %copy-done), channel_id=1, source_target_pairs={{0,20},{1,21},{2,22},{3,23},{4,16},{5,17},{6,18},{7,19},{8,28},{9,... | collective-permute-start | bytes 786440 | tf_op jit(solution)/shard_map/ppermute | solution.py:408
  23.8 4.6 %collective-permute-start.8 = (bf16[128,1024]{1,0:T(8,128)(2,1)S(1)}, bf16[128,1024]{1,0:T(8,128)(2,1)S(1)}, u32[]{:S(2)}, u32[]{:S(2)}) collective-permute-start(bf16[128,1024]{1,0:T(8,128)(2,1)S(1)} %collective-permute-done.6.refs_6_.refs_8_), channel_id=1, source_target_pairs={{0,4},{1,5},{2,6},{3,7},{4,0},{5,1},{6,2},{7,3},{8,12},{9,13},{10,... | collective-permute-start | bytes 786440 | tf_op jit(solution)/shard_map/ppermute | solution.py:408
  24.2 4.2 %collective-permute-start.9 = (bf16[128,1024]{1,0:T(8,128)(2,1)S(1)}, bf16[128,1024]{1,0:T(8,128)(2,1)S(1)}, u32[]{:S(2)}, u32[]{:S(2)}) collective-permute-start(bf16[128,1024]{1,0:T(8,128)(2,1)S(1)} %collective-permute-done.7.refs_7_.refs_9_), channel_id=1, source_target_pairs={{0,4},{1,5},{2,6},{3,7},{4,0},{5,1},{6,2},{7,3},{8,12},{9,13},{10,... | collective-permute-start | bytes 786440 | tf_op jit(solution)/shard_map/ppermute | solution.py:408
  24.3 8.7 %collective-permute-start.11 = (bf16[128,1024]{1,0:T(8,128)(2,1)S(1)}, bf16[128,1024]{1,0:T(8,128)(2,1)S(1)}, u32[]{:S(2)}, u32[]{:S(2)}) collective-permute-start(bf16[128,1024]{1,0:T(8,128)(2,1)S(1)} %collective-permute-done.10.refs_4_.refs_12_), channel_id=1, source_target_pairs={{0,4},{1,5},{2,6},{3,7},{4,0},{5,1},{6,2},{7,3},{8,12},{9,13},{10,... | collective-permute-start | bytes 786440 | tf_op jit(solution)/shard_map/ppermute | solution.py:408
  24.7 7.3 %collective-permute-start.4 = (bf16[128,512]{1,0:T(8,128)(2,1)S(1)}, bf16[128,512]{1,0:T(8,128)(2,1)S(1)}, u32[]{:S(2)}, u32[]{:S(2)}) collective-permute-start(bf16[128,512]{1,0:T(8,128)(2,1)S(1)} %collective-permute-done.1.refs_1_), channel_id=1, source_target_pairs={{0,20},{1,21},{2,22},{3,23},{4,16},{5,17},{6,18},{7,19},{8,28},{9,... | collective-permute-start | bytes 393224 | tf_op jit(solution)/shard_map/ppermute | solution.py:408
  26.0 7.1 %collective-permute-start.5 = (bf16[128,512]{1,0:T(8,128)(2,1)S(1)}, bf16[128,512]{1,0:T(8,128)(2,1)S(1)}, u32[]{:S(2)}, u32[]{:S(2)}) collective-permute-start(bf16[128,512]{1,0:T(8,128)(2,1)S(1)} %collective-permute-done.2.refs_2_), channel_id=1, source_target_pairs={{0,20},{1,21},{2,22},{3,23},{4,16},{5,17},{6,18},{7,19},{8,28},{9,... | collective-permute-start | bytes 393224 | tf_op jit(solution)/shard_map/ppermute | solution.py:408
  26.5 0.7 %copy-start.1 = (s32[10]{0:T(128)S(1)}, s32[10]{0:T(128)}, u32[]{:S(2)}) copy-start(s32[10]{0:T(128)} %powers.1) | copy-start | bytes 124
  34.9 4.2 %collective-permute-start.12 = (f32[5,8,128]{2,1,0:T(8,128)S(1)}, f32[5,8,128]{2,1,0:T(8,128)S(1)}, u32[]{:S(2)}, u32[]{:S(2)}) collective-permute-start(f32[5,8,128]{2,1,0:T(8,128)S(1)} %shard_map.60), channel_id=1, source_target_pairs={{0,6},{1,7},{2,4},{3,5},{4,2},{5,3},{6,0},{7,1},{8,14},{9,15},{10,... | collective-permute-start | bytes 61448 | tf_op jit(solution)/shard_map/ppermute | solution.py:408
  39.0 3.2 %collective-permute-start.13 = (f32[5,8,128]{2,1,0:T(8,128)S(1)}, f32[5,8,128]{2,1,0:T(8,128)S(1)}, u32[]{:S(2)}, u32[]{:S(2)}) collective-permute-start(f32[5,8,128]{2,1,0:T(8,128)S(1)} %add.10), channel_id=1, source_target_pairs={{0,20},{1,21},{2,22},{3,23},{4,16},{5,17},{6,18},{7,19},{8,28},{9,... | collective-permute-start | bytes 61448 | tf_op jit(solution)/shard_map/ppermute | solution.py:408
  42.2 3.2 %collective-permute-start.14 = (f32[1,5,8,128]{3,2,1,0:T(8,128)S(1)}, f32[1,5,8,128]{3,2,1,0:T(8,128)S(1)}, u32[]{:S(2)}, u32[]{:S(2)}) collective-permute-start(f32[1,5,8,128]{3,2,1,0:T(8,128)S(1)} %bitcast.5), channel_id=1, source_target_pairs={{0,5},{1,4},{2,7},{3,6},{4,1},{5,0},{6,3},{7,2},{8,13},{9,12},{10,... | collective-permute-start | bytes 61448 | tf_op jit(solution)/shard_map/ppermute | solution.py:408
  45.5 3.6 %collective-permute-start.15 = (f32[2,5,8,128]{3,2,1,0:T(8,128)S(1)}, f32[2,5,8,128]{3,2,1,0:T(8,128)S(1)}, u32[]{:S(2)}, u32[]{:S(2)}) collective-permute-start(f32[2,5,8,128]{3,2,1,0:T(8,128)S(1)} %pad_maximum_fusion.2), channel_id=1, source_target_pairs={{0,12},{1,13},{2,14},{3,15},{4,8},{5,9},{6,10},{7,11},{8,4},{9,5},... | collective-permute-start | bytes 122888 | tf_op jit(solution)/shard_map/ppermute | solution.py:408
  49.1 1.3 %collective-permute-start.16 = (f32[4,5,8,128]{3,2,1,0:T(8,128)S(1)}, f32[4,5,8,128]{3,2,1,0:T(8,128)S(1)}, u32[]{:S(2)}, u32[]{:S(2)}) collective-permute-start(f32[4,5,8,128]{3,2,1,0:T(8,128)S(1)} %pad_maximum_fusion.1), channel_id=1, source_target_pairs={{0,4},{1,5},{2,6},{3,7},{4,0},{5,1},{6,2},{7,3},{8,12},{9,13},{10,... | collective-permute-start | bytes 245768 | tf_op jit(solution)/shard_map/ppermute | solution.py:408

commit v4 on v3

--- a/solution.py
+++ b/solution.py
@@ -396,6 +396,13 @@
     return [bit ^ cols for bit in far], [bit ^ cols for bit in near]
 
 
+def span(bits):
+    masks = [0]
+    for bit in bits:
+        masks += [mask ^ bit for mask in masks]
+    return masks
+
+
 def on_device(expression, powers):
     rows, cols = lax.axis_size("row"), lax.axis_size("col")
     devices = rows * cols
@@ -421,7 +428,10 @@
     place = jnp.broadcast_to(mine, (TILE, genes))
 
     width = samples // PIECES
-    pieces = tuple(expression[:, i * width : (i + 1) * width] for i in range(PIECES))
+    pieces, source = [], expression
+    for i in range(PIECES):
+        pieces.append(source[:, i * width : (i + 1) * width])
+        source = lax.optimization_barrier(source)
     lane_blocks = [(expression,)]
     for i, bit in enumerate(far):
         sent = [pieces] if i == 0 else lane_blocks
@@ -449,12 +459,30 @@
     ready = known + new + second
     part = late_sums(scales, place, here, last, ready, third, stats, part)
 
-    for bit in far:
-        part = part + from_partner(part, bit)
+    def hops(array, bits):
+        return [array] + [from_partner(array, mask) for mask in span(bits)[1:]]
+
+    def tree_sum(parts):
+        while len(parts) > 1:
+            parts = [parts[i] + parts[i + 1] for i in range(0, len(parts), 2)]
+        return parts[0]
+
+    def in_order(parts, flags):
+        for up in flags:
+            pairs = [(parts[i], parts[i + 1]) for i in range(0, len(parts), 2)]
+            parts = [
+                jnp.concatenate([jnp.where(up, high, low), jnp.where(up, low, high)])
+                for low, high in pairs
+            ]
+        return parts[0]
+
+    for i in range(len(far) - 1, -1, -1):
+        part = tree_sum(hops(part, far[i : i + 1]))
     own, part = part, part[None]
-    for bit, up in zip(near + [core], upper):
-        got = from_partner(part, bit)
-        part = jnp.concatenate([jnp.where(up, got, part), jnp.where(up, part, got)])
+    for i in range(0, len(near), 2):
+        bits = near[i : i + 2]
+        part = in_order(hops(part, bits), upper[i : i + len(bits)])
+    part = in_order(hops(part, [core]), upper[-1:])
 
     log_degree, degree_freq, fit_slope, mean_log = fit(npower, len(lane_blocks), place, part, own)
     return log_degree, degree_freq, fit_slope[0], mean_log[0]

time: 51.9 us -> 50.9 us (0.981)
  waiting for transfers between devices: 20.6 us -> 18.7 us
  starting transfers between devices: 20.8 us -> 21.7 us
    ppermute x17 -> x18, waiting for transfers between devices: 20.6 us -> 18.7 us  [from_partner(): return lax.ppermute(array, AXES, [(i, i ^ bit) for i in range(devices)])]
    ppermute x17 -> x18, starting transfers between devices: 20.8 us -> 21.7 us  [from_partner(): return lax.ppermute(array, AXES, [(i, i ^ bit) for i in range(devices)])]
  transfers between devices with their start and end apart: 17 -> 18, of which waited for: 8 -> 8; matrix products, arithmetic and copies ran while one was open for 2% -> 2% of each run, Pallas kernels for 9% -> 9%
where the time goes in v4:
time: 50.9 us; the launch traced here: 50.7 us
  starting transfers between devices  21.7 us (43%)
  waiting for transfers between devices  18.7 us (37%)
  Pallas kernels  7.8 us (15%)
  local copies, waits for them, and re-layouts  1.62 us (3%)
  between operations  0.79 us (2%)
    ppermute x18, starting transfers between devices, from_partner(): return lax.ppermute(array, AXES, [(i, i ^ bit) for i in range(devices)])  21.7 us
    ppermute x18, waiting for transfers between devices, from_partner(): return lax.ppermute(array, AXES, [(i, i ^ bit) for i in range(devices)])  18.7 us
    pallas_call x5, Pallas kernels, pallas(): pl.pallas_call(kernel, out_shape=out_shape, in_specs=[pl.BlockSpec(memory...  7.8 us
  transfers between devices with their start and end apart: 18, of which 8 were waited for; matrix products, arithmetic and copies ran while one was open for 2% of the time, Pallas kernels for 9%

profile of v4, /device:TPU:0, one launch (start us, length us, event | category | flops | bytes accessed | tf_op | source)
XLA Modules:
  0.0 50.7 jit_solution(9240287424895525742)
XLA Ops:
  0.6 0.0 copy-start
  0.6 2.6 %collective-permute-start.6 = (bf16[128,1024]{1,0:T(8,128)(2,1)}, bf16[128,1024]{1,0:T(8,128)(2,1)S(1)}, u32[]{:S(2)}, u32[]{:S(2)}) collective-permute-start(bf16[128,1024]{1,0:T(8,128)(2,1)} %refs_6_.1), channel_id=1, source_target_pairs={{0,5},{1,4},{2,7},{3,6},{4,1},{5,0},{6,3},{7,2},{8,13},{9,12},{10,... | collective-permute-start | bytes 786440 | tf_op jit(solution)/shard_map/ppermute | solution.py:415
  3.2 1.8 %collective-permute-start.7 = (bf16[128,1024]{1,0:T(8,128)(2,1)}, bf16[128,1024]{1,0:T(8,128)(2,1)S(1)}, u32[]{:S(2)}, u32[]{:S(2)}) collective-permute-start(bf16[128,1024]{1,0:T(8,128)(2,1)} %refs_6_.1), channel_id=1, source_target_pairs={{0,12},{1,13},{2,14},{3,15},{4,8},{5,9},{6,10},{7,11},{8,4},{9,5},... | collective-permute-start | bytes 786440 | tf_op jit(solution)/shard_map/ppermute | solution.py:415
  5.0 0.9 %slice.6 = bf16[128,512]{1,0:T(8,128)(2,1)S(1)} slice(bf16[128,1024]{1,0:T(8,128)(2,1)} %refs_6_.1), slice={[0:128], [0:512]} | slice | bytes 262144 | tf_op jit(solution)/shard_map/slice | solution.py:433
  5.9 2.1 %collective-permute-start.1 = (bf16[128,512]{1,0:T(8,128)(2,1)S(1)}, bf16[128,512]{1,0:T(8,128)(2,1)S(1)}, u32[]{:S(2)}, u32[]{:S(2)}) collective-permute-start(bf16[128,512]{1,0:T(8,128)(2,1)S(1)} %slice.6), channel_id=1, source_target_pairs={{0,6},{1,7},{2,4},{3,5},{4,2},{5,3},{6,0},{7,1},{8,14},{9,15},{10,... | collective-permute-start | bytes 393224 | tf_op jit(solution)/shard_map/ppermute | solution.py:415
  8.0 2.2 %collective-permute-done.6.refs_6_.refs_8_ = bf16[128,1024]{1,0:T(8,128)(2,1)S(1)} collective-permute-done((bf16[128,1024]{1,0:T(8,128)(2,1)}, bf16[128,1024]{1,0:T(8,128)(2,1)S(1)}, u32[]{:S(2)}, u32[]{:S(2)}) %collective-permute-start.6) | collective-permute-done | bytes 262176 | tf_op jit(solution)/shard_map/ppermute | solution.py:415
  10.2 4.7 %collective-permute-start.10 = (bf16[128,1024]{1,0:T(8,128)(2,1)S(1)}, bf16[128,1024]{1,0:T(8,128)(2,1)S(1)}, u32[]{:S(2)}, u32[]{:S(2)}) collective-permute-start(bf16[128,1024]{1,0:T(8,128)(2,1)S(1)} %collective-permute-done.6.refs_6_.refs_8_), channel_id=1, source_target_pairs={{0,12},{1,13},{2,14},{3,15},{4,8},{5,9},{6,10},{7,11},{8,4},{9,5},... | collective-permute-start | bytes 786440 | tf_op jit(solution)/shard_map/ppermute | solution.py:415
  14.9 0.0 copy-done
  14.9 2.0 %collective-permute-start.2 = (bf16[128,512]{1,0:T(8,128)(2,1)S(1)}, bf16[128,512]{1,0:T(8,128)(2,1)S(1)}, u32[]{:S(2)}, u32[]{:S(2)}) collective-permute-start(bf16[128,512]{1,0:T(8,128)(2,1)S(1)} %slice.8), channel_id=1, source_target_pairs={{0,6},{1,7},{2,4},{3,5},{4,2},{5,3},{6,0},{7,1},{8,14},{9,15},{10,... | collective-permute-start | bytes 393224 | tf_op jit(solution)/shard_map/ppermute | solution.py:415
  16.9 0.1 collective-permute-start
  17.0 0.0 collective-permute-done.1.refs_1_
  17.0 1.5 %collective-permute-start.3 = (bf16[128,1024]{1,0:T(8,128)(2,1)S(1)}, bf16[128,1024]{1,0:T(8,128)(2,1)S(1)}, u32[]{:S(2)}, u32[]{:S(2)}) collective-permute-start(bf16[128,1024]{1,0:T(8,128)(2,1)S(1)} %copy-done), channel_id=1, source_target_pairs={{0,20},{1,21},{2,22},{3,23},{4,16},{5,17},{6,18},{7,19},{8,28},{9,... | collective-permute-start | bytes 786440 | tf_op jit(solution)/shard_map/ppermute | solution.py:415
  18.5 5.4 %collective-permute-done.2.refs_2_ = bf16[128,512]{1,0:T(8,128)(2,1)S(1)} collective-permute-done((bf16[128,512]{1,0:T(8,128)(2,1)S(1)}, bf16[128,512]{1,0:T(8,128)(2,1)S(1)}, u32[]{:S(2)}, u32[]{:S(2)}) %collective-permute-start.2) | collective-permute-done | bytes 131104 | tf_op jit(solution)/shard_map/ppermute | solution.py:415
  23.9 0.4 collective-permute-start.8
  24.3 0.0 collective-permute-done.7.refs_7_.refs_9_
  24.3 0.1 collective-permute-start.9
  24.4 0.0 collective-permute-done.10.refs_4_.refs_12_
  24.4 0.4 collective-permute-start.11
  24.8 0.0 collective-permute-done.refs_1_.refs_5_.refs_7_
  24.8 1.2 %collective-permute-start.4 = (bf16[128,512]{1,0:T(8,128)(2,1)S(1)}, bf16[128,512]{1,0:T(8,128)(2,1)S(1)}, u32[]{:S(2)}, u32[]{:S(2)}) collective-permute-start(bf16[128,512]{1,0:T(8,128)(2,1)S(1)} %collective-permute-done.1.refs_1_), channel_id=1, source_target_pairs={{0,20},{1,21},{2,22},{3,23},{4,16},{5,17},{6,18},{7,19},{8,28},{9,... | collective-permute-start | bytes 393224 | tf_op jit(solution)/shard_map/ppermute | solution.py:415
  26.1 0.0 collective-permute-done.3.refs_3_
  26.1 0.5 %collective-permute-start.5 = (bf16[128,512]{1,0:T(8,128)(2,1)S(1)}, bf16[128,512]{1,0:T(8,128)(2,1)S(1)}, u32[]{:S(2)}, u32[]{:S(2)}) collective-permute-start(bf16[128,512]{1,0:T(8,128)(2,1)S(1)} %collective-permute-done.2.refs_2_), channel_id=1, source_target_pairs={{0,20},{1,21},{2,22},{3,23},{4,16},{5,17},{6,18},{7,19},{8,28},{9,... | collective-permute-start | bytes 393224 | tf_op jit(solution)/shard_map/ppermute | solution.py:415
  26.6 0.0 copy-start.1
  26.6 0.7 %copy-done.1 = s32[10]{0:T(128)S(1)} copy-done((s32[10]{0:T(128)S(1)}, s32[10]{0:T(128)}, u32[]{:S(2)}) %copy-start.1) | copy-done | bytes 64
  27.2 1.2 %shard_map.57 = (f32[10,8,128]{2,1,0:T(8,128)S(1)}, f32[1,12,128]{2,1,0:T(8,128)S(1)}, f32[2,2,128,128]{3,2,1,0:T(8,128)S(1)}) custom-call(s32[10]{0:T(128)S(1)} %copy-done.1, bf16[128,1024]{1,0:T(8,128)(2,1)S(1)} %copy-done, bf16[128,1024]{1,0:T(8,128)(2,1)S(1)} %copy-done, bf16[128,1024]{1,0:T(8,128)(2,1)S(1)} %collective-permute-done.refs_1_.refs_5_.refs_7_), custom_call_target="tpu_custom_call" | custom-call | flops 67108864 | bytes 131072 | tf_op jit(solution)/shard_map/pallas_call | solution.py:40
  28.5 0.0 collective-permute-done.8.refs_8_.refs_10_
  28.5 0.0 collective-permute-done.9.refs_9_.refs_11_
  28.5 2.9 %shard_map.58 = (f32[3,12,128]{2,1,0:T(8,128)S(1)}, f32[4,2,128,128]{3,2,1,0:T(8,128)S(1)}) custom-call(f32[10,8,128]{2,1,0:T(8,128)S(1)} %get-tuple-element.15.scales, s32[8,128]{1,0:T(8,128)S(1)} %broadcast_in_dim.6.place, bf16[128,1024]{1,0:T(8,128)(2,1)S(1)} %copy-done, bf16[128,512]{1,0:T(8,128)(2,1)S(1)} %collective-permute-done.1.refs_1_, ...), custom_call_target="tpu_custom_call" | custom-call | flops 603979776 | bytes 1179648 | tf_op jit(solution)/shard_map/pallas_call | solution.py:40
  31.4 0.7 %shard_map.59 = (f32[3,12,128]{2,1,0:T(8,128)S(1)}, f32[1,2,128,128]{3,2,1,0:T(8,128)S(1)}) custom-call(f32[10,8,128]{2,1,0:T(8,128)S(1)} %get-tuple-element.15.scales, s32[8,128]{1,0:T(8,128)S(1)} %broadcast_in_dim.6.place, bf16[128,1024]{1,0:T(8,128)(2,1)S(1)} %copy-done, bf16[128,512]{1,0:T(8,128)(2,1)S(1)} %collective-permute-done.1.refs_1_, ...), custom_call_target="tpu_custom_call" | custom-call | flops 100663296 | bytes 196608 | tf_op jit(solution)/shard_map/pallas_call | solution.py:40
  32.1 0.0 collective-permute-done.4.refs_4_
  32.1 1.0 %collective-permute-done.5.refs_5_ = bf16[128,512]{1,0:T(8,128)(2,1)S(1)} collective-permute-done((bf16[128,512]{1,0:T(8,128)(2,1)S(1)}, bf16[128,512]{1,0:T(8,128)(2,1)S(1)}, u32[]{:S(2)}, u32[]{:S(2)}) %collective-permute-start.5) | collective-permute-done | bytes 131104 | tf_op jit(solution)/shard_map/ppermute | solution.py:415
  33.1 0.0 collective-permute-done.11.refs_13_
  33.1 1.8 %shard_map.60 = f32[5,8,128]{2,1,0:T(8,128)S(1)} custom-call(f32[10,8,128]{2,1,0:T(8,128)S(1)} %get-tuple-element.15.scales, s32[8,128]{1,0:T(8,128)S(1)} %broadcast_in_dim.6.place, bf16[128,1024]{1,0:T(8,128)(2,1)S(1)} %copy-done, bf16[128,512]{1,0:T(8,128)(2,1)S(1)} %collective-permute-done.1.refs_1_, bf16[128,512]{1,0:T(8,128)(2,1)S(1)} %collective-permute-done.2.refs_2_, ...), custom_call_target="tpu_custom_call" | custom-call | flops 369098752 | bytes 720896 | tf_op jit(solution)/shard_map/pallas_call | solution.py:40
  34.9 1.3 %collective-permute-start.12 = (f32[5,8,128]{2,1,0:T(8,128)S(1)}, f32[5,8,128]{2,1,0:T(8,128)S(1)}, u32[]{:S(2)}, u32[]{:S(2)}) collective-permute-start(f32[5,8,128]{2,1,0:T(8,128)S(1)} %shard_map.60), channel_id=1, source_target_pairs={{0,20},{1,21},{2,22},{3,23},{4,16},{5,17},{6,18},{7,19},{8,28},{9,... | collective-permute-start | bytes 61448 | tf_op jit(solution)/shard_map/ppermute | solution.py:415
  36.2 2.0 %collective-permute-done.12 = f32[5,8,128]{2,1,0:T(8,128)S(1)} collective-permute-done((f32[5,8,128]{2,1,0:T(8,128)S(1)}, f32[5,8,128]{2,1,0:T(8,128)S(1)}, u32[]{:S(2)}, u32[]{:S(2)}) %collective-permute-start.12) | collective-permute-done | bytes 20512 | tf_op jit(solution)/shard_map/ppermute | solution.py:415
  38.2 0.0 collective-permute-start.13
  38.2 4.1 %collective-permute-done.13 = f32[5,8,128]{2,1,0:T(8,128)S(1)} collective-permute-done((f32[5,8,128]{2,1,0:T(8,128)S(1)}, f32[5,8,128]{2,1,0:T(8,128)S(1)}, u32[]{:S(2)}, u32[]{:S(2)}) %collective-permute-start.13) | collective-permute-done | bytes 20512 | tf_op jit(solution)/shard_map/ppermute | solution.py:415
  42.3 1.1 %collective-permute-start.16 = (f32[1,5,8,128]{3,2,1,0:T(8,128)S(1)}, f32[1,5,8,128]{3,2,1,0:T(8,128)S(1)}, u32[]{:S(2)}, u32[]{:S(2)}) collective-permute-start(f32[1,5,8,128]{3,2,1,0:T(8,128)S(1)} %bitcast.5), channel_id=1, source_target_pairs={{0,5},{1,4},{2,7},{3,6},{4,1},{5,0},{6,3},{7,2},{8,13},{9,12},{10,... | collective-permute-start | bytes 61448 | tf_op jit(solution)/shard_map/ppermute | solution.py:415
  43.4 0.4 collective-permute-start.14
  43.8 1.4 %collective-permute-start.15 = (f32[1,5,8,128]{3,2,1,0:T(8,128)S(1)}, f32[1,5,8,128]{3,2,1,0:T(8,128)S(1)}, u32[]{:S(2)}, u32[]{:S(2)}) collective-permute-start(f32[1,5,8,128]{3,2,1,0:T(8,128)S(1)} %bitcast.7), channel_id=1, source_target_pairs={{0,12},{1,13},{2,14},{3,15},{4,8},{5,9},{6,10},{7,11},{8,4},{9,5},... | collective-permute-start | bytes 61448 | tf_op jit(solution)/shard_map/ppermute | solution.py:415
  45.3 0.3 collective-permute-done.16
  45.5 2.5 %collective-permute-done.14 = f32[1,5,8,128]{3,2,1,0:T(8,128)S(1)} collective-permute-done((f32[1,5,8,128]{3,2,1,0:T(8,128)S(1)}, f32[1,5,8,128]{3,2,1,0:T(8,128)S(1)}, u32[]{:S(2)}, u32[]{:S(2)}) %collective-permute-start.14) | collective-permute-done | bytes 20512 | tf_op jit(solution)/shard_map/ppermute | solution.py:415
  48.1 0.0 collective-permute-done.15
  48.1 0.1 collective-permute-start.17
  48.2 1.2 %collective-permute-done.17 = f32[4,5,8,128]{3,2,1,0:T(8,128)S(1)} collective-permute-done((f32[4,5,8,128]{3,2,1,0:T(8,128)S(1)}, f32[4,5,8,128]{3,2,1,0:T(8,128)S(1)}, u32[]{:S(2)}, u32[]{:S(2)}) %collective-permute-start.17) | collective-permute-done | bytes 81952 | tf_op jit(solution)/shard_map/ppermute | solution.py:415
  49.5 1.2 %shard_map.61 = (f32[10,128]{1,0:T(8,128)}, f32[10,10]{1,0:T(8,128)}, f32[1,10]{1,0:T(1,128)}, f32[1,10]{1,0:T(1,128)}) custom-call(s32[8,128]{1,0:T(8,128)S(1)} %broadcast_in_dim.6.place, f32[8,5,8,128]{3,2,1,0:T(8,128)S(1)} %pad_maximum_fusion.deg, f32[5,8,128]{2,1,0:T(8,128)S(1)} %add.11.own), custom_call_target="tpu_custom_call" | custom-call | tf_op jit(solution)/shard_map/pallas_call | solution.py:40
  (10 shorter events, 0.1 us)
Async XLA Ops:
  0.6 14.3 %copy-start = (bf16[128,1024]{1,0:T(8,128)(2,1)S(1)}, bf16[128,1024]{1,0:T(8,128)(2,1)}, u32[]{:S(2)}) copy-start(bf16[128,1024]{1,0:T(8,128)(2,1)} %refs_6_.1) | copy-start | bytes 786436
  0.6 9.6 %collective-permute-start.6 = (bf16[128,1024]{1,0:T(8,128)(2,1)}, bf16[128,1024]{1,0:T(8,128)(2,1)S(1)}, u32[]{:S(2)}, u32[]{:S(2)}) collective-permute-start(bf16[128,1024]{1,0:T(8,128)(2,1)} %refs_6_.1), channel_id=1, source_target_pairs={{0,5},{1,4},{2,7},{3,6},{4,1},{5,0},{6,3},{7,2},{8,13},{9,12},{10,... | collective-permute-start | bytes 786440 | tf_op jit(solution)/shard_map/ppermute | solution.py:415
  3.2 21.1 %collective-permute-start.7 = (bf16[128,1024]{1,0:T(8,128)(2,1)}, bf16[128,1024]{1,0:T(8,128)(2,1)S(1)}, u32[]{:S(2)}, u32[]{:S(2)}) collective-permute-start(bf16[128,1024]{1,0:T(8,128)(2,1)} %refs_6_.1), channel_id=1, source_target_pairs={{0,12},{1,13},{2,14},{3,15},{4,8},{5,9},{6,10},{7,11},{8,4},{9,5},... | collective-permute-start | bytes 786440 | tf_op jit(solution)/shard_map/ppermute | solution.py:415
  5.9 11.1 %collective-permute-start.1 = (bf16[128,512]{1,0:T(8,128)(2,1)S(1)}, bf16[128,512]{1,0:T(8,128)(2,1)S(1)}, u32[]{:S(2)}, u32[]{:S(2)}) collective-permute-start(bf16[128,512]{1,0:T(8,128)(2,1)S(1)} %slice.6), channel_id=1, source_target_pairs={{0,6},{1,7},{2,4},{3,5},{4,2},{5,3},{6,0},{7,1},{8,14},{9,15},{10,... | collective-permute-start | bytes 393224 | tf_op jit(solution)/shard_map/ppermute | solution.py:415
  10.2 14.2 %collective-permute-start.10 = (bf16[128,1024]{1,0:T(8,128)(2,1)S(1)}, bf16[128,1024]{1,0:T(8,128)(2,1)S(1)}, u32[]{:S(2)}, u32[]{:S(2)}) collective-permute-start(bf16[128,1024]{1,0:T(8,128)(2,1)S(1)} %collective-permute-done.6.refs_6_.refs_8_), channel_id=1, source_target_pairs={{0,12},{1,13},{2,14},{3,15},{4,8},{5,9},{6,10},{7,11},{8,4},{9,5},... | collective-permute-start | bytes 786440 | tf_op jit(solution)/shard_map/ppermute | solution.py:415
  14.9 9.0 %collective-permute-start.2 = (bf16[128,512]{1,0:T(8,128)(2,1)S(1)}, bf16[128,512]{1,0:T(8,128)(2,1)S(1)}, u32[]{:S(2)}, u32[]{:S(2)}) collective-permute-start(bf16[128,512]{1,0:T(8,128)(2,1)S(1)} %slice.8), channel_id=1, source_target_pairs={{0,6},{1,7},{2,4},{3,5},{4,2},{5,3},{6,0},{7,1},{8,14},{9,15},{10,... | collective-permute-start | bytes 393224 | tf_op jit(solution)/shard_map/ppermute | solution.py:415
  16.9 7.9 %collective-permute-start = (bf16[128,1024]{1,0:T(8,128)(2,1)S(1)}, bf16[128,1024]{1,0:T(8,128)(2,1)S(1)}, u32[]{:S(2)}, u32[]{:S(2)}) collective-permute-start(bf16[128,1024]{1,0:T(8,128)(2,1)S(1)} %copy-done), channel_id=1, source_target_pairs={{0,4},{1,5},{2,6},{3,7},{4,0},{5,1},{6,2},{7,3},{8,12},{9,13},{10,... | collective-permute-start | bytes 786440 | tf_op jit(solution)/shard_map/ppermute | solution.py:415
  17.0 9.1 %collective-permute-start.3 = (bf16[128,1024]{1,0:T(8,128)(2,1)S(1)}, bf16[128,1024]{1,0:T(8,128)(2,1)S(1)}, u32[]{:S(2)}, u32[]{:S(2)}) collective-permute-start(bf16[128,1024]{1,0:T(8,128)(2,1)S(1)} %copy-done), channel_id=1, source_target_pairs={{0,20},{1,21},{2,22},{3,23},{4,16},{5,17},{6,18},{7,19},{8,28},{9,... | collective-permute-start | bytes 786440 | tf_op jit(solution)/shard_map/ppermute | solution.py:415
  23.9 4.6 %collective-permute-start.8 = (bf16[128,1024]{1,0:T(8,128)(2,1)S(1)}, bf16[128,1024]{1,0:T(8,128)(2,1)S(1)}, u32[]{:S(2)}, u32[]{:S(2)}) collective-permute-start(bf16[128,1024]{1,0:T(8,128)(2,1)S(1)} %collective-permute-done.6.refs_6_.refs_8_), channel_id=1, source_target_pairs={{0,4},{1,5},{2,6},{3,7},{4,0},{5,1},{6,2},{7,3},{8,12},{9,13},{10,... | collective-permute-start | bytes 786440 | tf_op jit(solution)/shard_map/ppermute | solution.py:415
  24.3 4.2 %collective-permute-start.9 = (bf16[128,1024]{1,0:T(8,128)(2,1)S(1)}, bf16[128,1024]{1,0:T(8,128)(2,1)S(1)}, u32[]{:S(2)}, u32[]{:S(2)}) collective-permute-start(bf16[128,1024]{1,0:T(8,128)(2,1)S(1)} %collective-permute-done.7.refs_7_.refs_9_), channel_id=1, source_target_pairs={{0,4},{1,5},{2,6},{3,7},{4,0},{5,1},{6,2},{7,3},{8,12},{9,13},{10,... | collective-permute-start | bytes 786440 | tf_op jit(solution)/shard_map/ppermute | solution.py:415
  24.4 8.7 %collective-permute-start.11 = (bf16[128,1024]{1,0:T(8,128)(2,1)S(1)}, bf16[128,1024]{1,0:T(8,128)(2,1)S(1)}, u32[]{:S(2)}, u32[]{:S(2)}) collective-permute-start(bf16[128,1024]{1,0:T(8,128)(2,1)S(1)} %collective-permute-done.10.refs_4_.refs_12_), channel_id=1, source_target_pairs={{0,4},{1,5},{2,6},{3,7},{4,0},{5,1},{6,2},{7,3},{8,12},{9,13},{10,... | collective-permute-start | bytes 786440 | tf_op jit(solution)/shard_map/ppermute | solution.py:415
  24.8 7.3 %collective-permute-start.4 = (bf16[128,512]{1,0:T(8,128)(2,1)S(1)}, bf16[128,512]{1,0:T(8,128)(2,1)S(1)}, u32[]{:S(2)}, u32[]{:S(2)}) collective-permute-start(bf16[128,512]{1,0:T(8,128)(2,1)S(1)} %collective-permute-done.1.refs_1_), channel_id=1, source_target_pairs={{0,20},{1,21},{2,22},{3,23},{4,16},{5,17},{6,18},{7,19},{8,28},{9,... | collective-permute-start | bytes 393224 | tf_op jit(solution)/shard_map/ppermute | solution.py:415
  26.1 7.1 %collective-permute-start.5 = (bf16[128,512]{1,0:T(8,128)(2,1)S(1)}, bf16[128,512]{1,0:T(8,128)(2,1)S(1)}, u32[]{:S(2)}, u32[]{:S(2)}) collective-permute-start(bf16[128,512]{1,0:T(8,128)(2,1)S(1)} %collective-permute-done.2.refs_2_), channel_id=1, source_target_pairs={{0,20},{1,21},{2,22},{3,23},{4,16},{5,17},{6,18},{7,19},{8,28},{9,... | collective-permute-start | bytes 393224 | tf_op jit(solution)/shard_map/ppermute | solution.py:415
  26.6 0.7 %copy-start.1 = (s32[10]{0:T(128)S(1)}, s32[10]{0:T(128)}, u32[]{:S(2)}) copy-start(s32[10]{0:T(128)} %powers.1) | copy-start | bytes 124
  34.9 3.3 %collective-permute-start.12 = (f32[5,8,128]{2,1,0:T(8,128)S(1)}, f32[5,8,128]{2,1,0:T(8,128)S(1)}, u32[]{:S(2)}, u32[]{:S(2)}) collective-permute-start(f32[5,8,128]{2,1,0:T(8,128)S(1)} %shard_map.60), channel_id=1, source_target_pairs={{0,20},{1,21},{2,22},{3,23},{4,16},{5,17},{6,18},{7,19},{8,28},{9,... | collective-permute-start | bytes 61448 | tf_op jit(solution)/shard_map/ppermute | solution.py:415
  38.2 4.1 %collective-permute-start.13 = (f32[5,8,128]{2,1,0:T(8,128)S(1)}, f32[5,8,128]{2,1,0:T(8,128)S(1)}, u32[]{:S(2)}, u32[]{:S(2)}) collective-permute-start(f32[5,8,128]{2,1,0:T(8,128)S(1)} %add.10), channel_id=1, source_target_pairs={{0,6},{1,7},{2,4},{3,5},{4,2},{5,3},{6,0},{7,1},{8,14},{9,15},{10,... | collective-permute-start | bytes 61448 | tf_op jit(solution)/shard_map/ppermute | solution.py:415
  42.3 3.2 %collective-permute-start.16 = (f32[1,5,8,128]{3,2,1,0:T(8,128)S(1)}, f32[1,5,8,128]{3,2,1,0:T(8,128)S(1)}, u32[]{:S(2)}, u32[]{:S(2)}) collective-permute-start(f32[1,5,8,128]{3,2,1,0:T(8,128)S(1)} %bitcast.5), channel_id=1, source_target_pairs={{0,5},{1,4},{2,7},{3,6},{4,1},{5,0},{6,3},{7,2},{8,13},{9,12},{10,... | collective-permute-start | bytes 61448 | tf_op jit(solution)/shard_map/ppermute | solution.py:415
  43.4 4.7 %collective-permute-start.14 = (f32[1,5,8,128]{3,2,1,0:T(8,128)S(1)}, f32[1,5,8,128]{3,2,1,0:T(8,128)S(1)}, u32[]{:S(2)}, u32[]{:S(2)}) collective-permute-start(f32[1,5,8,128]{3,2,1,0:T(8,128)S(1)} %bitcast.6), channel_id=1, source_target_pairs={{0,9},{1,8},{2,11},{3,10},{4,13},{5,12},{6,15},{7,14},{8,1},{9,0},... | collective-permute-start | bytes 61448 | tf_op jit(solution)/shard_map/ppermute | solution.py:415
  43.8 4.3 %collective-permute-start.15 = (f32[1,5,8,128]{3,2,1,0:T(8,128)S(1)}, f32[1,5,8,128]{3,2,1,0:T(8,128)S(1)}, u32[]{:S(2)}, u32[]{:S(2)}) collective-permute-start(f32[1,5,8,128]{3,2,1,0:T(8,128)S(1)} %bitcast.7), channel_id=1, source_target_pairs={{0,12},{1,13},{2,14},{3,15},{4,8},{5,9},{6,10},{7,11},{8,4},{9,5},... | collective-permute-start | bytes 61448 | tf_op jit(solution)/shard_map/ppermute | solution.py:415
  48.1 1.3 %collective-permute-start.17 = (f32[4,5,8,128]{3,2,1,0:T(8,128)S(1)}, f32[4,5,8,128]{3,2,1,0:T(8,128)S(1)}, u32[]{:S(2)}, u32[]{:S(2)}) collective-permute-start(f32[4,5,8,128]{3,2,1,0:T(8,128)S(1)} %pad_maximum_fusion.1), channel_id=1, source_target_pairs={{0,4},{1,5},{2,6},{3,7},{4,0},{5,1},{6,2},{7,3},{8,12},{9,13},{10,... | collective-permute-start | bytes 245768 | tf_op jit(solution)/shard_map/ppermute | solution.py:415
